TPU v7x, 256 devices: a whole 4x4x8 slice. The times are simulated.
256 devices in a mesh: tm: 8 (over x, core), space: 32 (over z, y).
Axes of the slice: x: 4, y: 4, z: 8, core: 2. Of those that a mesh axis runs over, the one named last changes fastest.
Arguments:
- span_opening: float32 [8, 128, 64, 128], P('tm', 'space'), may hold values from -8 to 8
- source_power: float32 [8, 2, 128, 64, 128], P('tm', None, 'space'), may hold values from -24 to 24
- warmth_retention: float32 [128, 64, 128], P('space'), may hold values from 0.02 to 0.4
Outputs:
- fpoint: float32 [8, 128, 64, 128], P('tm', 'space')
- updated: float32 [8, 128, 64, 128], P('tm', 'space')
All inputs are finite; a program needn't handle non-finite values.
Results may differ from a plain program's by a relative error of at most 0.0001.
Values sent between devices are 32-bit elements; how exact they have to be, the bound alone decides.
A program may use at most 64 MiB of HBM per device.

v0:
```python
import functools

import jax
import jax.numpy as jnp
from jax import lax
from jax.experimental import pallas as pl
from jax.experimental.pallas import tpu as pltpu
from jax.sharding import PartitionSpec as P

COARSE_SWEEPS = 24
W = 0.8
F32 = jnp.float32
MESH = pl.DeviceIdType.MESH


def iota(shape, dim):
    return lax.broadcasted_iota(jnp.int32, shape, dim)


def dot(a, b):
    total = None
    for _ in range(3):
        part = a.astype(jnp.bfloat16)
        a = a - part.astype(F32)
        term = jnp.dot(part, b, preferred_element_type=F32)
        total = term if total is None else total + term
    return total


def picks(lanes, pick, scale):
    src, dst = iota((lanes, lanes), 0), iota((lanes, lanes), 1)
    return jnp.where(pick(src, dst), scale, 0.0).astype(jnp.bfloat16)


def in_plane(x, width):
    rows, lanes = x.shape[1], x.shape[2]
    lane, row = iota(x.shape, 2), iota(x.shape, 1)
    left, right = pltpu.roll(x, 1, 2), pltpu.roll(x, lanes - 1, 2)
    if width > lanes // 4:
        left = jnp.where(lane % width == 0, 0.0, left)
        right = jnp.where(lane % width == width - 1, 0.0, right)
    up = jnp.where(row == 0, 0.0, pltpu.roll(x, 1, 1))
    down = jnp.where(row == rows - 1, 0.0, pltpu.roll(x, rows - 1, 1))
    return (left + right) + (up + down)


def shifted(x):
    zero = jnp.zeros((1,) + x.shape[1:], F32)
    return jnp.concatenate([zero, x[:-1]], 0), jnp.concatenate([x[1:], zero], 0)


def sum_planes(x, width):
    before, after = shifted(x)
    return in_plane(x, width) + (before + after)


def sum_packed(x, width):
    half = pltpu.roll(x, width, 2)
    before, after = shifted(half)
    return in_plane(x, width) + (half + jnp.where(iota(x.shape, 2) < width, before, after))


def sum_inner(x, width):
    return in_plane(x[1:-1], width) + (x[:-2] + x[2:])


def column_sum(x):
    rows = x.shape[1]
    row = iota(x.shape, 1)
    before, after = shifted(x)
    up = jnp.where(row == 0, 0.0, pltpu.roll(x, 1, 1))
    down = jnp.where(row == rows - 1, 0.0, pltpu.roll(x, rows - 1, 1))
    return (before + after) + (up + down)


def coarse_solve(c, a, lanes):
    def moved(x):
        return pltpu.roll(x, 1, 2), x, pltpu.roll(x, lanes - 1, 2)

    cs, as_ = moved(c), moved(a)

    def two_sweeps(_, y):
        far = pltpu.roll(y, 2, 2), pltpu.roll(y, lanes - 2, 2)
        near = moved(y)
        sides = far[0] + y, near[0] + near[2], y + far[1]
        once = [
            (0.2 * y_at + c_at) + a_at * (side + column_sum(y_at))
            for y_at, c_at, a_at, side in zip(near, cs, as_, sides)
        ]
        return (0.2 * once[1] + c) + a * ((once[0] + once[2]) + column_sum(once[1]))

    left = COARSE_SWEEPS - 1
    y = c
    if left % 2:
        y = 1.2 * c + a * sum_planes(c, lanes // 8)
    return lax.fori_loop(0, left // 2, two_sweeps, y, unroll=True)


def flat(x):
    return x.reshape(x.shape[0] * x.shape[1], x.shape[2])


def kernel(
    parts, spans, steps,
    open_ref, src_ref, cap_in,
    fp_ref, up_ref,
    u0, src0, src1, cap, c0, c1x, gcap, gr, own, x1p, tmp, fin,
    in_sem, hs, hr, ks, kr, fs, fr, gs, gv, ts,
):
    me, span = lax.axis_index("space"), lax.axis_index("tm")
    depth, rows, lanes = open_ref.shape
    half = lanes // 2

    barrier = pltpu.get_barrier_semaphore()
    for k in range(1, parts):
        pl.semaphore_signal(barrier, inc=1, device_id={"space": (me + k) % parts}, device_id_type=MESH)
    for k in range(1, spans):
        pl.semaphore_signal(barrier, inc=1, device_id={"tm": (span + k) % spans}, device_id_type=MESH)

    loads = [
        pltpu.make_async_copy(cap_in, cap.at[pl.ds(depth, depth)], in_sem.at[0]),
        pltpu.make_async_copy(open_ref, u0, in_sem.at[1]),
        pltpu.make_async_copy(src_ref.at[0], src0, in_sem.at[2]),
        pltpu.make_async_copy(src_ref.at[1], src1.at[pl.ds(2, depth)], in_sem.at[3]),
    ]
    for load in loads:
        load.start()

    down_lo = picks(lanes, lambda s, d: (s // 2 == d) & (d < half), 0.125)
    down_hi = picks(lanes, lambda s, d: s // 2 + half == d, 0.125)
    down_2 = picks(lanes, lambda s, d: (s % half) // 2 == d, 0.125)
    down_3 = picks(lanes, lambda s, d: (s // 2 == d) & (s < half // 2), 0.125)
    up_lo = picks(lanes, lambda s, d: d // 2 == s, 1.0)
    up_hi = picks(lanes, lambda s, d: d // 2 + half == s, 1.0)
    up_2 = picks(lanes, lambda s, d: (d % half) // 2 == s, 1.0)
    up_3 = picks(lanes, lambda s, d: (d // 2 == s) & (d < half // 2), 1.0)

    def pair_rows(x):
        n, r, w = x.shape
        tmp[pl.ds(0, n * r), :] = flat(x)
        return tmp[pl.ds(0, n * r // 2, 2), :] + tmp[pl.ds(1, n * r // 2, 2), :]

    def twice_rows(x, planes):
        r = x.shape[0]
        tmp[pl.ds(0, r, 2), :] = x
        tmp[pl.ds(1, r, 2), :] = x
        return tmp[pl.ds(0, 2 * r), :].reshape(planes, 2 * r // planes, lanes)

    def pack(x):
        s = pair_rows(x.reshape(depth // 2, 2, rows, lanes).sum(1))
        n = rows // 2
        return dot(s[:n], down_lo) + dot(s[n:], down_hi)

    def to_2(x):
        return dot(pair_rows(x), down_2).reshape(parts, rows // 4, lanes)

    def to_3(x):
        s = x.reshape(parts // 2, 2, rows // 4, lanes).sum(1)
        return dot(pair_rows(s), down_3).reshape(parts // 2, rows // 8, lanes)

    def halo(buf, sends, recvs, at, count, up, down, reach=1, rows_at=None):
        def cut(start):
            return buf.at[pl.ds(start, count)] if rows_at is None else buf.at[pl.ds(start, count), rows_at]

        ways = ((up, reach, at), (down, parts - reach, at + 1))
        pair = [
            pltpu.make_async_remote_copy(
                cut(way[0]), cut(way[1]), sends.at[sem], recvs.at[sem],
                device_id={"space": (me + by) % parts}, device_id_type=MESH)
            for way, by, sem in ways
        ]
        return pair + [reach]

    def begin(pair):
        @pl.when(me < parts - pair[2])
        def _():
            pair[0].start()

        @pl.when(me >= pair[2])
        def _():
            pair[1].start()

    def arrive(pair):
        @pl.when(me >= pair[2])
        def _():
            pair[0].wait_recv()

        @pl.when(me < parts - pair[2])
        def _():
            pair[1].wait_recv()

    def sent(pair):
        @pl.when(me < parts - pair[2])
        def _():
            pair[0].wait_send()

        @pl.when(me >= pair[2])
        def _():
            pair[1].wait_send()

    share = rows // spans
    my_rows = pl.ds(pl.multiple_of(span * share, share), share)

    def hand_on(at, count, below, above):
        def copies(start, sem):
            return [
                pltpu.make_async_remote_copy(
                    cap.at[pl.ds(start, count), my_rows], cap.at[pl.ds(start, count), my_rows],
                    fs.at[sem, k], fr.at[sem, k],
                    device_id={"tm": (span + k) % spans}, device_id_type=MESH)
                for k in range(1, spans)
            ]

        return copies(below, at), copies(above, at + 1)

    def each(pair, act):
        @pl.when(me > 0)
        def _():
            for copy in pair[0]:
                act(copy)

        @pl.when(me < parts - 1)
        def _():
            for copy in pair[1]:
                act(copy)

    def gather(buf, sends, recvs, row):
        return [
            pltpu.make_async_remote_copy(
                buf.at[me], buf.at[me], sends.at[row, k], recvs.at[row, k],
                device_id={"space": (me + k) % parts}, device_id_type=MESH)
            for k in range(1, parts)
        ]

    d = depth
    near = halo(c0, hs, hr, 0, 2, (2 * d - 1, d - 1), (d + 1, 2 * d + 1))
    far = halo(c0, hs, hr, 2, d - 2, (d + 1, 1), (d + 3, 2 * d + 3))
    beyond = halo(c0, hs, hr, 4, 1, (2 * d, 0), (d + 1, 3 * d + 1), reach=2)
    source = halo(src1, hs, hr, 6, 2, (d, 0), (2, d + 2))
    third = halo(c1x, hs, hr, 8, 1, (d, 0), (5, d + 5))
    cap_near = halo(cap, ks, kr, 0, 1, (2 * d - 1, d - 1), (d, 2 * d), rows_at=my_rows)
    cap_far = halo(cap, ks, kr, 2, d - 1, (d, 0), (d + 1, 2 * d + 1), rows_at=my_rows)
    pass_near = hand_on(0, 1, d - 1, 2 * d)
    pass_far = hand_on(2, d - 1, 0, 2 * d + 1)
    gather_cap = gather(gcap, gs, gv, 0)
    gather_r = [gather(gr.at[t], gs, gv, 1 + t) for t in range(steps)]

    def clear(ref, start, stop):
        ref[start:stop] = jnp.zeros((stop - start, rows, lanes), F32)

    @pl.when(me == 0)
    def _():
        clear(cap, 0, d)
        clear(c0, 0, d + 1)
        clear(c1x, 0, 3)
        clear(src1, 0, 2)

    @pl.when(me == 1)
    def _():
        clear(c0, 0, 1)

    @pl.when(me == parts - 2)
    def _():
        clear(c0, 3 * d + 1, 3 * d + 2)

    @pl.when(me == parts - 1)
    def _():
        clear(cap, 2 * d, 3 * d)
        clear(c0, 2 * d + 1, 3 * d + 2)
        clear(c1x, d + 3, d + 6)
        clear(src1, d + 2, d + 4)

    x1p[0] = jnp.zeros(x1p.shape[1:], F32)
    x1p[parts + 1] = jnp.zeros(x1p.shape[1:], F32)

    loads[0].wait()
    mine = cap[d:2 * d]
    gcap[me] = pack(mine)
    loads[1].wait()
    loads[2].wait()
    b = mine * u0[...] + src0[...]
    own[...] = b
    c0[d + 1:2 * d + 1] = b * (W / (mine + 6.0))
    loads[3].wait()

    pl.semaphore_wait(barrier, parts - 1 + spans - 1)
    begin(cap_near)
    begin(near)
    for copy in gather_cap:
        copy.start()

    def weights(start, count):
        plane = (me - 1) * depth + start + iota((count, 1, 1), 0)
        inside = (plane >= 0) & (plane < parts * depth)
        return jnp.where(inside, W / (cap[start:start + count] + 6.0), 0.0)

    arrive(cap_near)
    each(pass_near, lambda copy: copy.start())
    each(pass_near, lambda copy: copy.wait_recv())
    a = weights(d - 1, d + 2)

    for t in range(steps):
        if t == 0:
            arrive(near)
            c = c0[d - 1:2 * d + 3]
        else:
            c = c1x[1:d + 5]
        x = 1.2 * c[1:-1] + a * sum_inner(c, lanes)
        inner = x[1:-1]
        d0 = cap[d:2 * d] + 6.0
        r = own[...] - d0 * inner + sum_inner(x, lanes)
        gr[t, me] = pack(r)
        for copy in gather_r[t]:
            copy.start()
        if t == 1:
            begin(third)
        else:
            begin(cap_far)
            begin(far)
            begin(beyond)
            begin(source)
            for copy in gather_cap:
                copy.wait_recv()
            cap1 = gcap[...]
            i1 = W / (cap1 + 3.0)
            cap2 = to_2(cap1)
            i2 = jnp.where(iota(cap2.shape, 2) < lanes // 4, W / (cap2 + 1.5), 0.0)
            cap3 = to_3(cap2)
            i3 = jnp.where(iota(cap3.shape, 2) < lanes // 8, W / (cap3 + 0.75), 0.0)
            a1, a2, a3 = 0.5 * i1, 0.25 * i2, 0.125 * i3

        for copy in gather_r[t]:
            copy.wait_recv()
        b1 = gr[t]
        c1 = b1 * i1
        y1 = 1.2 * c1 + a1 * sum_packed(c1, half)
        r1 = b1 - (cap1 + 3.0) * y1 + 0.5 * sum_packed(y1, half)
        b2 = to_2(r1)
        c2 = b2 * i2
        y2 = 1.2 * c2 + a2 * sum_planes(c2, lanes // 4)
        r2 = b2 - (cap2 + 1.5) * y2 + 0.25 * sum_planes(y2, lanes // 4)
        c3 = to_3(r2) * i3
        if t == 0:
            arrive(cap_far)
            each(pass_far, lambda copy: copy.start())
        y3 = coarse_solve(c3, a3, lanes)
        lift = twice_rows(dot(flat(y3), up_3), parts // 2)
        lift = jnp.broadcast_to(lift[:, None], (parts // 2, 2) + lift.shape[1:]).reshape(y2.shape)
        y2 = y2 + lift
        for _ in range(2):
            y2 = (0.2 * y2 + c2) + a2 * sum_planes(y2, lanes // 4)
        y1 = y1 + twice_rows(dot(flat(y2), up_2), parts)
        for _ in range(2):
            y1 = (0.2 * y1 + c1) + a1 * sum_packed(y1, half)
        x1p[1:parts + 1] = y1

        n = rows // 2
        around = flat(x1p[pl.ds(me, 3)])
        even, odd = dot(around, up_lo), dot(around, up_hi)
        halves = [part[n * k:n * k + n] for k in range(3) for part in (even, odd)]
        if t == 1:
            halves = halves[1:-1]
        planes = len(halves)
        lift = twice_rows(jnp.concatenate(halves, 0), planes)
        lift = jnp.broadcast_to(lift[:, None], (planes, 2) + lift.shape[1:]).reshape(2 * planes, rows, lanes)
        if t == 0:
            each(pass_far, lambda copy: copy.wait_recv())
            arrive(far)
            arrive(beyond)
            a_lo, a_hi = weights(0, d - 1), weights(2 * d + 1, d - 1)
            first = 1.2 * c0[1:d] + a_lo * sum_inner(c0[0:d + 1], lanes)
            final = 1.2 * c0[2 * d + 2:3 * d + 1] + a_hi * sum_inner(c0[2 * d + 1:3 * d + 2], lanes)
            wide = jnp.concatenate([a_lo, a, a_hi], 0)
            x = jnp.concatenate([first, x, final], 0) + lift
            x = (0.2 * x[1:-1] + c0[2:3 * d]) + wide[1:-1] * sum_inner(x, lanes)
            x = (0.2 * x[1:-1] + c0[3:3 * d - 1]) + wide[2:-2] * sum_inner(x, lanes)
            fp_ref[...] = x[2:-2]
            arrive(source)
            b = cap[2:3 * d - 2] * x + src1[...]
            own[...] = b[2:-2]
            c1x[1:d + 5] = b * wide[2:-2]
        else:
            arrive(third)
            first = 1.2 * c1x[1:2] + wide[2:3] * sum_inner(c1x[0:3], lanes)
            final = 1.2 * c1x[d + 4:d + 5] + wide[-3:-2] * sum_inner(c1x[d + 3:d + 6], lanes)
            x = jnp.concatenate([first, x, final], 0) + lift
            x = (0.2 * x[1:-1] + c1x[2:d + 4]) + a * sum_inner(x, lanes)
            fin[...] = (0.2 * x[1:-1] + c1x[3:d + 3]) + a[1:-1] * sum_inner(x, lanes)

    onward = pltpu.make_async_remote_copy(
        fin, up_ref, ts.at[0], ts.at[1],
        device_id={"tm": (span + 1) % spans}, device_id_type=MESH)

    @pl.when(span < spans - 1)
    def _():
        onward.start()

    @pl.when(span == 0)
    def _():
        up_ref[...] = u0[...]

    for pair in (near, far, beyond, source, third, cap_near, cap_far):
        sent(pair)
    for pair in (pass_near, pass_far):
        each(pair, lambda copy: copy.wait_send())
    for copies in [gather_cap] + gather_r:
        for copy in copies:
            copy.wait_send()

    @pl.when(span < spans - 1)
    def _():
        onward.wait_send()

    @pl.when(span > 0)
    def _():
        onward.wait_recv()


def shards(span_opening, source_power, warmth_retention):
    parts, spans = lax.axis_size("space"), lax.axis_size("tm")
    steps = source_power.shape[1]
    depth, rows, lanes = warmth_retention.shape
    assert steps == 2 and depth == 4
    slab = jax.ShapeDtypeStruct((depth, rows, lanes), F32)
    vmem = pl.BlockSpec(memory_space=pltpu.VMEM)
    dma = pltpu.SemaphoreType.DMA
    fpoint, updated = pl.pallas_call(
        functools.partial(kernel, parts, spans, steps),
        out_shape=(pltpu.VMEM(slab.shape, F32),) * 2,
        in_specs=[pl.BlockSpec(memory_space=pl.ANY)] * 3,
        out_specs=(vmem, vmem),
        scratch_shapes=[
            pltpu.VMEM((depth, rows, lanes), F32),
            pltpu.VMEM((depth, rows, lanes), F32),
            pltpu.VMEM((depth + 4, rows, lanes), F32),
            pltpu.VMEM((3 * depth, rows, lanes), F32),
            pltpu.VMEM((3 * depth + 2, rows, lanes), F32),
            pltpu.VMEM((depth + 6, rows, lanes), F32),
            pltpu.VMEM((parts, rows // 2, lanes), F32),
            pltpu.VMEM((steps, parts, rows // 2, lanes), F32),
            pltpu.VMEM((depth, rows, lanes), F32),
            pltpu.VMEM((parts + 2, rows // 2, lanes), F32),
            pltpu.VMEM((max(parts * rows // 2, 6 * rows), lanes), F32),
            pltpu.VMEM((depth, rows, lanes), F32),
            dma((4,)), dma((10,)), dma((10,)), dma((4,)), dma((4,)), dma((4, spans)), dma((4, spans)),
            dma((1 + steps, parts)), dma((1 + steps, parts)), dma((2,)),
        ],
        compiler_params=pltpu.CompilerParams(
            collective_id=0, has_side_effects=True, vmem_limit_bytes=67043328 - 2 * 4 * slab.size
        ),
    )(span_opening[0], source_power[0], warmth_retention)
    return fpoint[None], updated[None]


def solution(mesh):
    in_specs = (
        P("tm", "space", None, None),
        P("tm", None, "space", None, None),
        P("space", None, None),
    )
    out_specs = (P("tm", "space", None, None), P("tm", "space", None, None))
    return jax.shard_map(shards, mesh=mesh, in_specs=in_specs, out_specs=out_specs, check_vma=False)
```

profile of v0, /device:TPU:1, one launch (start us, length us, event | category | flops | bytes accessed | tf_op | source)
XLA Modules:
  0.0 74.6 jit_solution(16183590336912772451)
XLA Ops:
  0.6 72.6 %shard_map.50 = (f32[4,64,128]{2,1,0:T(8,128)S(1)}, f32[4,64,128]{2,1,0:T(8,128)S(1)}) custom-call(f32[4,64,128]{2,1,0:T(8,128)} %bitcast.7, f32[2,4,64,128]{3,2,1,0:T(8,128)} %bitcast.6, f32[4,64,128]{2,1,0:T(8,128)} %cap_in.1), custom_call_target="tpu_custom_call" | custom-call | tf_op jit(solution)/shard_map/pallas_call | solution.py:427
  73.3 0.7 copy.7
  73.9 0.7 copy.8
where the time goes:
time: 74.7 us; the launch traced here: 74.6 us
  Pallas kernels  72.6 us (97%)
  local copies, waits for them, and re-layouts  1.31 us (2%)
    pallas_call x1, Pallas kernels, shards(): pl.pallas_call(functools.partial(kernel, parts, spans, steps), out_shape=...  72.6 us

commit v1 on v0

--- a/solution.py
+++ b/solution.py
@@ -9,6 +9,8 @@
 
 COARSE_SWEEPS = 24
 W = 0.8
+GROUP = 32
+NEAR = (1, 2, 3, 4, 8, 12)
 F32 = jnp.float32
 MESH = pl.DeviceIdType.MESH
 
@@ -36,9 +38,8 @@
     rows, lanes = x.shape[1], x.shape[2]
     lane, row = iota(x.shape, 2), iota(x.shape, 1)
     left, right = pltpu.roll(x, 1, 2), pltpu.roll(x, lanes - 1, 2)
-    if width > lanes // 4:
-        left = jnp.where(lane % width == 0, 0.0, left)
-        right = jnp.where(lane % width == width - 1, 0.0, right)
+    left = jnp.where(lane % width == 0, 0.0, left)
+    right = jnp.where(lane % width == width - 1, 0.0, right)
     up = jnp.where(row == 0, 0.0, pltpu.roll(x, 1, 1))
     down = jnp.where(row == rows - 1, 0.0, pltpu.roll(x, rows - 1, 1))
     return (left + right) + (up + down)
@@ -49,9 +50,28 @@
     return jnp.concatenate([zero, x[:-1]], 0), jnp.concatenate([x[1:], zero], 0)
 
 
-def sum_planes(x, width):
-    before, after = shifted(x)
-    return in_plane(x, width) + (before + after)
+def earlier(x, by=1, shift=0):
+    lanes = x.shape[2]
+    moved = pltpu.roll(x[-by:], (GROUP + shift) % lanes, 2)
+    return jnp.where(iota(moved.shape, 2) < GROUP, 0.0, moved)
+
+
+def later(x, by=1, shift=0):
+    lanes = x.shape[2]
+    moved = pltpu.roll(x[:by], (lanes - GROUP + shift) % lanes, 2)
+    return jnp.where(iota(moved.shape, 2) >= lanes - GROUP, 0.0, moved)
+
+
+def before(x):
+    return jnp.concatenate([earlier(x), x[:-1]], 0)
+
+
+def after(x):
+    return jnp.concatenate([x[1:], later(x)], 0)
+
+
+def sum_grouped(x):
+    return in_plane(x, GROUP) + (before(x) + after(x))
 
 
 def sum_packed(x, width):
@@ -66,33 +86,38 @@
 
 def column_sum(x):
     rows = x.shape[1]
-    row = iota(x.shape, 1)
-    before, after = shifted(x)
-    up = jnp.where(row == 0, 0.0, pltpu.roll(x, 1, 1))
-    down = jnp.where(row == rows - 1, 0.0, pltpu.roll(x, rows - 1, 1))
-    return (before + after) + (up + down)
-
-
-def coarse_solve(c, a, lanes):
-    def moved(x):
-        return pltpu.roll(x, 1, 2), x, pltpu.roll(x, lanes - 1, 2)
-
-    cs, as_ = moved(c), moved(a)
+    mid = x[1:-1]
+    row = iota(mid.shape, 1)
+    up = jnp.where(row == 0, 0.0, pltpu.roll(mid, 1, 1))
+    down = jnp.where(row == rows - 1, 0.0, pltpu.roll(mid, rows - 1, 1))
+    return (x[:-2] + x[2:]) + (up + down)
+
+
+def coarse_solve(c, a):
+    n, lanes = c.shape[0], c.shape[2]
+
+    def turned(x, by):
+        return x if by == 0 else pltpu.roll(x, by % lanes, 2)
+
+    def longer(x, by, reach=1):
+        return jnp.concatenate([earlier(x, reach, by), turned(x, by), later(x, reach, by)], 0)
+
+    c_at, a_at = [[longer(x, 0) if by == 0 else turned(x, by) for by in (1, 0, -1)] for x in (c, a)]
+
+    def sweep(y, side, c, a):
+        return (0.2 * y[1:-1] + c) + a * (side + column_sum(y))
 
     def two_sweeps(_, y):
-        far = pltpu.roll(y, 2, 2), pltpu.roll(y, lanes - 2, 2)
-        near = moved(y)
-        sides = far[0] + y, near[0] + near[2], y + far[1]
-        once = [
-            (0.2 * y_at + c_at) + a_at * (side + column_sum(y_at))
-            for y_at, c_at, a_at, side in zip(near, cs, as_, sides)
-        ]
-        return (0.2 * once[1] + c) + a * ((once[0] + once[2]) + column_sum(once[1]))
+        left, mid, right = longer(y, 1), longer(y, 0, 2), longer(y, -1)
+        once_left = sweep(left, turned(y, 2) + y, c_at[0], a_at[0])
+        once_mid = sweep(mid, left + right, c_at[1], a_at[1])
+        once_right = sweep(right, y + turned(y, -2), c_at[2], a_at[2])
+        return sweep(once_mid, once_left + once_right, c, a)
 
     left = COARSE_SWEEPS - 1
     y = c
     if left % 2:
-        y = 1.2 * c + a * sum_planes(c, lanes // 8)
+        y = 1.2 * c + a * sum_grouped(c)
     return lax.fori_loop(0, left // 2, two_sweeps, y, unroll=True)
 
 
@@ -104,15 +129,23 @@
     parts, spans, steps,
     open_ref, src_ref, cap_in,
     fp_ref, up_ref,
-    u0, src0, src1, cap, c0, c1x, gcap, gr, own, x1p, tmp, fin,
-    in_sem, hs, hr, ks, kr, fs, fr, gs, gv, ts,
+    u0, src0, src1, cap, c0, c1x, cw, vw, gr, y2s, own, tmp, fin,
+    far_sem, in_sem, hs, hr, ks, kr, fs, fr, gs, gv, ws, wr, ts,
 ):
     me, span = lax.axis_index("space"), lax.axis_index("tm")
     depth, rows, lanes = open_ref.shape
     half = lanes // 2
+    groups = lanes // GROUP
+    stack = parts // groups
+    assert parts % groups == 0 and lanes == 128 and rows == 64
+    close = sorted({k % parts for k in NEAR} | {-k % parts for k in NEAR})
+    assert {(a + b) % parts for a in close + [0] for b in close + [0]} == set(range(parts))
+
+    cw[...] = jnp.zeros(cw.shape, F32)
+    vw[...] = jnp.zeros(vw.shape, F32)
 
     barrier = pltpu.get_barrier_semaphore()
-    for k in range(1, parts):
+    for k in close:
         pl.semaphore_signal(barrier, inc=1, device_id={"space": (me + k) % parts}, device_id_type=MESH)
     for k in range(1, spans):
         pl.semaphore_signal(barrier, inc=1, device_id={"tm": (span + k) % spans}, device_id_type=MESH)
@@ -126,14 +159,18 @@
     for load in loads:
         load.start()
 
+    group = me // stack
     down_lo = picks(lanes, lambda s, d: (s // 2 == d) & (d < half), 0.125)
     down_hi = picks(lanes, lambda s, d: s // 2 + half == d, 0.125)
-    down_2 = picks(lanes, lambda s, d: (s % half) // 2 == d, 0.125)
-    down_3 = picks(lanes, lambda s, d: (s // 2 == d) & (s < half // 2), 0.125)
+    down_2 = [
+        picks(lanes, lambda s, d: (s % half) // 2 + GROUP * ((group + q) % groups) == d, 0.125)
+        for q in range(groups)
+    ]
+    down_3 = picks(lanes, lambda s, d: s // GROUP * GROUP + s % GROUP // 2 == d, 0.125)
     up_lo = picks(lanes, lambda s, d: d // 2 == s, 1.0)
     up_hi = picks(lanes, lambda s, d: d // 2 + half == s, 1.0)
     up_2 = picks(lanes, lambda s, d: (d % half) // 2 == s, 1.0)
-    up_3 = picks(lanes, lambda s, d: (d // 2 == s) & (d < half // 2), 1.0)
+    up_3 = picks(lanes, lambda s, d: d // GROUP * GROUP + d % GROUP // 2 == s, 1.0)
 
     def pair_rows(x):
         n, r, w = x.shape
@@ -151,12 +188,46 @@
         n = rows // 2
         return dot(s[:n], down_lo) + dot(s[n:], down_hi)
 
-    def to_2(x):
-        return dot(pair_rows(x), down_2).reshape(parts, rows // 4, lanes)
+    def to_2(x, q):
+        return dot(pair_rows(x), down_2[q])
 
     def to_3(x):
-        s = x.reshape(parts // 2, 2, rows // 4, lanes).sum(1)
-        return dot(pair_rows(s), down_3).reshape(parts // 2, rows // 8, lanes)
+        s = x.reshape(stack // 2, 2, rows // 4, lanes).sum(1)
+        return dot(pair_rows(s), down_3).reshape(stack // 2, rows // 8, lanes)
+
+    def unpack(x, q):
+        at = (iota((stack,) + x.shape[1:], 2) // GROUP + groups - q) % groups
+        out = x[:stack]
+        for g in range(1, groups):
+            out = jnp.where(at == g, x[g * stack:(g + 1) * stack], out)
+        return pltpu.roll(out, lanes - GROUP * q, 2) if q else out
+
+    def within(k):
+        return (me + k >= 0) & (me + k < parts)
+
+    def window(buf, sends, recvs, reach):
+        middle = buf.shape[0] // 2
+        return [
+            (k, pltpu.make_async_remote_copy(
+                buf.at[middle], buf.at[middle - k], sends.at[middle + k], recvs.at[middle + k],
+                device_id={"space": (me + k + parts) % parts}, device_id_type=MESH))
+            for far in range(1, reach + 1) for k in (far, -far)
+        ]
+
+    def where_within(copies, sign, act):
+        for k, copy in copies:
+            @pl.when(within(sign * k))
+            def _(copy=copy):
+                act(copy)
+
+    def window_start(copies):
+        where_within(copies, 1, lambda copy: copy.start())
+
+    def window_arrive(copies):
+        where_within(copies, -1, lambda copy: copy.wait_recv())
+
+    def window_sent(copies):
+        where_within(copies, 1, lambda copy: copy.wait_send())
 
     def halo(buf, sends, recvs, at, count, up, down, reach=1, rows_at=None):
         def cut(start):
@@ -224,12 +295,16 @@
             for copy in pair[1]:
                 act(copy)
 
-    def gather(buf, sends, recvs, row):
+    def hops(k):
+        z, y = k // 4, k % 4
+        return min(z, parts // 4 - z) + min(y, 4 - y)
+
+    def gather(buf, sends, recvs):
         return [
             pltpu.make_async_remote_copy(
-                buf.at[me], buf.at[me], sends.at[row, k], recvs.at[row, k],
+                buf.at[me], buf.at[me], sends.at[k], recvs.at[k],
                 device_id={"space": (me + k) % parts}, device_id_type=MESH)
-            for k in range(1, parts)
+            for k in sorted(range(1, parts), key=lambda k: -hops(k))
         ]
 
     d = depth
@@ -238,12 +313,12 @@
     beyond = halo(c0, hs, hr, 4, 1, (2 * d, 0), (d + 1, 3 * d + 1), reach=2)
     source = halo(src1, hs, hr, 6, 2, (d, 0), (2, d + 2))
     third = halo(c1x, hs, hr, 8, 1, (d, 0), (5, d + 5))
-    cap_near = halo(cap, ks, kr, 0, 1, (2 * d - 1, d - 1), (d, 2 * d), rows_at=my_rows)
+    cap_near = halo(cap, ks, kr, 0, 1, (2 * d - 1, d - 1), (d, 2 * d))
     cap_far = halo(cap, ks, kr, 2, d - 1, (d, 0), (d + 1, 2 * d + 1), rows_at=my_rows)
-    pass_near = hand_on(0, 1, d - 1, 2 * d)
-    pass_far = hand_on(2, d - 1, 0, 2 * d + 1)
-    gather_cap = gather(gcap, gs, gv, 0)
-    gather_r = [gather(gr.at[t], gs, gv, 1 + t) for t in range(steps)]
+    pass_far = hand_on(0, d - 1, 0, 2 * d + 1)
+    gather_r = [gather(gr.at[t], gs.at[t], gv.at[t]) for t in range(steps)]
+    cap_window = window(cw, ws.at[0], wr.at[0], 2)
+    c_window = [window(vw.at[t], ws.at[1 + t], wr.at[1 + t], 3 - t) for t in range(steps)]
 
     def clear(ref, start, stop):
         ref[start:stop] = jnp.zeros((stop - start, rows, lanes), F32)
@@ -270,24 +345,27 @@
         clear(c1x, d + 3, d + 6)
         clear(src1, d + 2, d + 4)
 
-    x1p[0] = jnp.zeros(x1p.shape[1:], F32)
-    x1p[parts + 1] = jnp.zeros(x1p.shape[1:], F32)
-
     loads[0].wait()
     mine = cap[d:2 * d]
-    gcap[me] = pack(mine)
     loads[1].wait()
     loads[2].wait()
     b = mine * u0[...] + src0[...]
     own[...] = b
     c0[d + 1:2 * d + 1] = b * (W / (mine + 6.0))
+    cap1 = pack(mine)
+    cw[2] = cap1
     loads[3].wait()
 
-    pl.semaphore_wait(barrier, parts - 1 + spans - 1)
+    pl.semaphore_wait(barrier, len(close) + spans - 1)
+    begin(near)
     begin(cap_near)
-    begin(near)
-    for copy in gather_cap:
-        copy.start()
+    window_start(cap_window)
+    for k in close:
+        pl.semaphore_signal(far_sem, inc=1, device_id={"space": (me + k) % parts}, device_id_type=MESH)
+    begin(far)
+    begin(beyond)
+    begin(cap_far)
+    cap2_sent = to_2(cap1[None], groups - 1)
 
     def weights(start, count):
         plane = (me - 1) * depth + start + iota((count, 1, 1), 0)
@@ -295,8 +373,6 @@
         return jnp.where(inside, W / (cap[start:start + count] + 6.0), 0.0)
 
     arrive(cap_near)
-    each(pass_near, lambda copy: copy.start())
-    each(pass_near, lambda copy: copy.wait_recv())
     a = weights(d - 1, d + 2)
 
     for t in range(steps):
@@ -309,53 +385,77 @@
         inner = x[1:-1]
         d0 = cap[d:2 * d] + 6.0
         r = own[...] - d0 * inner + sum_inner(x, lanes)
-        gr[t, me] = pack(r)
+        b1 = pack(r)
+        if t == 0:
+            window_arrive(cap_window)
+            block = me - 2 + iota((5, 1, 1), 0)
+            d1 = cw[...] + 3.0
+            i1 = jnp.where((block >= 0) & (block < parts), W / d1, 0.0)
+            a1 = 0.5 * i1
+        c1 = b1 * i1[2]
+        vw[t, 3] = c1
+        none = jnp.zeros((1,) + b1.shape, F32)
+        c1 = jnp.concatenate([none, c1[None], none], 0)
+        y1 = 1.2 * c1 + a1[1:4] * sum_packed(c1, half)
+        r1 = jnp.concatenate([none, b1[None], none], 0) - d1[1:4] * y1 + 0.5 * sum_packed(y1, half)
+        parts_2 = to_2(r1[1:2], 0) + to_2(r1[0:1], 1) + to_2(r1[2:3], 2)
+        if t == 0:
+            parts_2 = parts_2 + cap2_sent
+            pl.semaphore_wait(far_sem, len(close))
+        gr[t, me] = parts_2
         for copy in gather_r[t]:
             copy.start()
+        window_start(c_window[t])
         if t == 1:
             begin(third)
         else:
-            begin(cap_far)
-            begin(far)
-            begin(beyond)
             begin(source)
-            for copy in gather_cap:
-                copy.wait_recv()
-            cap1 = gcap[...]
-            i1 = W / (cap1 + 3.0)
-            cap2 = to_2(cap1)
-            i2 = jnp.where(iota(cap2.shape, 2) < lanes // 4, W / (cap2 + 1.5), 0.0)
-            cap3 = to_3(cap2)
-            i3 = jnp.where(iota(cap3.shape, 2) < lanes // 8, W / (cap3 + 0.75), 0.0)
-            a1, a2, a3 = 0.5 * i1, 0.25 * i2, 0.125 * i3
+            arrive(cap_far)
+            each(pass_far, lambda copy: copy.start())
 
         for copy in gather_r[t]:
             copy.wait_recv()
-        b1 = gr[t]
-        c1 = b1 * i1
-        y1 = 1.2 * c1 + a1 * sum_packed(c1, half)
-        r1 = b1 - (cap1 + 3.0) * y1 + 0.5 * sum_packed(y1, half)
-        b2 = to_2(r1)
+        got = gr[t]
+        if t == 0:
+            cap2 = unpack(got, 3)
+            i2 = W / (cap2 + 1.5)
+            cap3 = to_3(cap2)
+            i3 = jnp.where(iota(cap3.shape, 2) % GROUP < GROUP // 2, W / (cap3 + 0.75), 0.0)
+            a2, a3 = 0.25 * i2, 0.125 * i3
+        b2 = unpack(got, 0) + after(unpack(got, 1)) + before(unpack(got, 2))
         c2 = b2 * i2
-        y2 = 1.2 * c2 + a2 * sum_planes(c2, lanes // 4)
-        r2 = b2 - (cap2 + 1.5) * y2 + 0.25 * sum_planes(y2, lanes // 4)
+        y2 = 1.2 * c2 + a2 * sum_grouped(c2)
+        r2 = b2 - (cap2 + 1.5) * y2 + 0.25 * sum_grouped(y2)
         c3 = to_3(r2) * i3
-        if t == 0:
-            arrive(cap_far)
-            each(pass_far, lambda copy: copy.start())
-        y3 = coarse_solve(c3, a3, lanes)
-        lift = twice_rows(dot(flat(y3), up_3), parts // 2)
-        lift = jnp.broadcast_to(lift[:, None], (parts // 2, 2) + lift.shape[1:]).reshape(y2.shape)
+        y3 = coarse_solve(c3, a3)
+        lift = twice_rows(dot(flat(y3), up_3), stack // 2)
+        lift = jnp.broadcast_to(lift[:, None], (stack // 2, 2) + lift.shape[1:]).reshape(y2.shape)
         y2 = y2 + lift
         for _ in range(2):
-            y2 = (0.2 * y2 + c2) + a2 * sum_planes(y2, lanes // 4)
-        y1 = y1 + twice_rows(dot(flat(y2), up_2), parts)
-        for _ in range(2):
+            y2 = (0.2 * y2 + c2) + a2 * sum_grouped(y2)
+        y2s[...] = y2
+        window_arrive(c_window[t])
+
+        lifts = []
+        for k in range(-2, 3):
+            at = (me + k + parts) % parts
+            plane = pltpu.roll(y2s[at % stack], (lanes - GROUP * (at // stack)) % lanes, 1)
+            lifts.append(jnp.where(within(k), plane, 0.0))
+        lift = twice_rows(dot(jnp.concatenate(lifts, 0), up_2), 5)
+        if t == 0:
+            c1 = vw[t]
+            y1 = 1.2 * c1[1:-1] + a1 * sum_packed(c1, half)[1:-1] + lift
+            c1 = c1[1:-1]
             y1 = (0.2 * y1 + c1) + a1 * sum_packed(y1, half)
-        x1p[1:parts + 1] = y1
+            y1 = ((0.2 * y1 + c1) + a1 * sum_packed(y1, half))[1:-1]
+        else:
+            c1 = vw[t, 1:6]
+            y1 = 1.2 * c1 + a1 * sum_packed(c1, half) + lift
+            y1 = ((0.2 * y1 + c1) + a1 * sum_packed(y1, half))[1:-1]
+            y1 = (0.2 * y1 + c1[1:-1]) + a1[1:-1] * sum_packed(y1, half)
 
         n = rows // 2
-        around = flat(x1p[pl.ds(me, 3)])
+        around = flat(y1)
         even, odd = dot(around, up_lo), dot(around, up_hi)
         halves = [part[n * k:n * k + n] for k in range(3) for part in (even, odd)]
         if t == 1:
@@ -401,9 +501,10 @@
 
     for pair in (near, far, beyond, source, third, cap_near, cap_far):
         sent(pair)
-    for pair in (pass_near, pass_far):
-        each(pair, lambda copy: copy.wait_send())
-    for copies in [gather_cap] + gather_r:
+    each(pass_far, lambda copy: copy.wait_send())
+    for copies in [cap_window] + c_window:
+        window_sent(copies)
+    for copies in gather_r:
         for copy in copies:
             copy.wait_send()
 
@@ -436,14 +537,16 @@
             pltpu.VMEM((3 * depth, rows, lanes), F32),
             pltpu.VMEM((3 * depth + 2, rows, lanes), F32),
             pltpu.VMEM((depth + 6, rows, lanes), F32),
-            pltpu.VMEM((parts, rows // 2, lanes), F32),
-            pltpu.VMEM((steps, parts, rows // 2, lanes), F32),
+            pltpu.VMEM((5, rows // 2, lanes), F32),
+            pltpu.VMEM((steps, 7, rows // 2, lanes), F32),
+            pltpu.VMEM((steps, parts, rows // 4, lanes), F32),
+            pltpu.VMEM((parts * GROUP // lanes, rows // 4, lanes), F32),
             pltpu.VMEM((depth, rows, lanes), F32),
-            pltpu.VMEM((parts + 2, rows // 2, lanes), F32),
-            pltpu.VMEM((max(parts * rows // 2, 6 * rows), lanes), F32),
+            pltpu.VMEM((6 * rows, lanes), F32),
             pltpu.VMEM((depth, rows, lanes), F32),
-            dma((4,)), dma((10,)), dma((10,)), dma((4,)), dma((4,)), dma((4, spans)), dma((4, spans)),
-            dma((1 + steps, parts)), dma((1 + steps, parts)), dma((2,)),
+            pltpu.SemaphoreType.REGULAR,
+            dma((4,)), dma((10,)), dma((10,)), dma((4,)), dma((4,)), dma((2, spans)), dma((2, spans)),
+            dma((steps, parts)), dma((steps, parts)), dma((1 + steps, 7)), dma((1 + steps, 7)), dma((2,)),
         ],
         compiler_params=pltpu.CompilerParams(
             collective_id=0, has_side_effects=True, vmem_limit_bytes=67043328 - 2 * 4 * slab.size

time: 74.7 us -> 46.2 us (0.62)
  Pallas kernels: 72.6 us -> 44.1 us
    pallas_call x1, Pallas kernels: 72.6 us -> 44.1 us  [shards(): pl.pallas_call(functools.partial(kernel, parts, spans, steps), out_shape=...]
where the time goes in v1:
time: 46.2 us; the launch traced here: 46.1 us
  Pallas kernels  44.1 us (95%)
  local copies, waits for them, and re-layouts  1.31 us (3%)
  between operations  0.64 us (1%)
    pallas_call x1, Pallas kernels, shards(): pl.pallas_call(functools.partial(kernel, parts, spans, steps), out_shape=...  44.1 us
    unnamed x2, local copies, waits for them, and re-layouts  1.31 us

profile of v1, /device:TPU:1, one launch (start us, length us, event | category | flops | bytes accessed | tf_op | source)
XLA Modules:
  0.0 46.1 jit_solution(4929525200088870524)
XLA Ops:
  0.6 44.1 %shard_map.50 = (f32[4,64,128]{2,1,0:T(8,128)S(1)}, f32[4,64,128]{2,1,0:T(8,128)S(1)}) custom-call(f32[4,64,128]{2,1,0:T(8,128)} %bitcast.7, f32[2,4,64,128]{3,2,1,0:T(8,128)} %bitcast.6, f32[4,64,128]{2,1,0:T(8,128)} %cap_in.1), custom_call_target="tpu_custom_call" | custom-call | tf_op jit(solution)/shard_map/pallas_call | solution.py:528
  44.8 0.7 %copy.7 = f32[1,4,64,128]{3,2,1,0:T(8,128)} copy(f32[1,4,64,128]{3,2,1,0:T(8,128)S(1)} %bitcast.5) | data formatting | bytes 262144
  45.4 0.7 %copy.8 = f32[1,4,64,128]{3,2,1,0:T(8,128)} copy(f32[1,4,64,128]{3,2,1,0:T(8,128)S(1)} %bitcast.4) | data formatting | bytes 262144

commit v2 on v1

--- a/solution.py
+++ b/solution.py
@@ -129,7 +129,7 @@
     parts, spans, steps,
     open_ref, src_ref, cap_in,
     fp_ref, up_ref,
-    u0, src0, src1, cap, c0, c1x, cw, vw, gr, y2s, own, tmp, fin,
+    u0, src0, src1, cap, c0, c1x, cw, vw, c_sent, gr, r_sent, y2s, own, tmp, fin,
     far_sem, in_sem, hs, hr, ks, kr, fs, fr, gs, gv, ws, wr, ts,
 ):
     me, span = lax.axis_index("space"), lax.axis_index("tm")
@@ -205,13 +205,13 @@
     def within(k):
         return (me + k >= 0) & (me + k < parts)
 
-    def window(buf, sends, recvs, reach):
+    def window(buf, source, sends, recvs, nearest, reach, to={}):
         middle = buf.shape[0] // 2
         return [
             (k, pltpu.make_async_remote_copy(
-                buf.at[middle], buf.at[middle - k], sends.at[middle + k], recvs.at[middle + k],
-                device_id={"space": (me + k + parts) % parts}, device_id_type=MESH))
-            for far in range(1, reach + 1) for k in (far, -far)
+                source, buf.at[middle - k], sends.at[middle + k], recvs.at[middle + k],
+                device_id={"space": (me + k + parts) % parts, **to}, device_id_type=MESH))
+            for far in range(nearest, reach + 1) for k in ((far, -far) if far else (0,))
         ]
 
     def where_within(copies, sign, act):
@@ -299,15 +299,16 @@
         z, y = k // 4, k % 4
         return min(z, parts // 4 - z) + min(y, 4 - y)
 
-    def gather(buf, sends, recvs):
+    def gather(source, target, sends, recvs, offsets, to):
         return [
             pltpu.make_async_remote_copy(
-                buf.at[me], buf.at[me], sends.at[k], recvs.at[k],
-                device_id={"space": (me + k) % parts}, device_id_type=MESH)
-            for k in sorted(range(1, parts), key=lambda k: -hops(k))
+                source, target, sends.at[k], recvs.at[k],
+                device_id={"space": (me + k) % parts, **to}, device_id_type=MESH)
+            for k in sorted(offsets, key=lambda k: -hops(k))
         ]
 
     d = depth
+    onward = {"tm": (span + 1) % spans}
     near = halo(c0, hs, hr, 0, 2, (2 * d - 1, d - 1), (d + 1, 2 * d + 1))
     far = halo(c0, hs, hr, 2, d - 2, (d + 1, 1), (d + 3, 2 * d + 3))
     beyond = halo(c0, hs, hr, 4, 1, (2 * d, 0), (d + 1, 3 * d + 1), reach=2)
@@ -316,9 +317,18 @@
     cap_near = halo(cap, ks, kr, 0, 1, (2 * d - 1, d - 1), (d, 2 * d))
     cap_far = halo(cap, ks, kr, 2, d - 1, (d, 0), (d + 1, 2 * d + 1), rows_at=my_rows)
     pass_far = hand_on(0, d - 1, 0, 2 * d + 1)
-    gather_r = [gather(gr.at[t], gs.at[t], gv.at[t]) for t in range(steps)]
-    cap_window = window(cw, ws.at[0], wr.at[0], 2)
-    c_window = [window(vw.at[t], ws.at[1 + t], wr.at[1 + t], 3 - t) for t in range(steps)]
+    gather_r = [
+        gather(gr.at[0, me], gr.at[0, me], gs.at[0], gv.at[0], range(1, parts), {}),
+        gather(r_sent, gr.at[1, me], gs.at[1], gv.at[1], range(parts), onward),
+    ]
+    cap_window = window(cw, cw.at[2], ws.at[0], wr.at[0], 1, 2)
+    c_window = [
+        window(vw.at[0], vw.at[0, 3], ws.at[1], wr.at[1], 1, 3),
+        window(vw.at[1], c_sent, ws.at[2], wr.at[2], 0, 2, onward),
+    ]
+    fin_onward = pltpu.make_async_remote_copy(
+        fin.at[0], fin.at[1], ts.at[0], ts.at[1],
+        device_id={"tm": (span + 1) % spans}, device_id_type=MESH)
 
     def clear(ref, start, stop):
         ref[start:stop] = jnp.zeros((stop - start, rows, lanes), F32)
@@ -372,56 +382,31 @@
         inside = (plane >= 0) & (plane < parts * depth)
         return jnp.where(inside, W / (cap[start:start + count] + 6.0), 0.0)
 
+    def inverse_1(start, stop):
+        block = me - 2 + start + iota((stop - start, 1, 1), 0)
+        diagonal = cw[start:stop] + 3.0
+        return diagonal, jnp.where((block >= 0) & (block < parts), W / diagonal, 0.0)
+
     arrive(cap_near)
     a = weights(d - 1, d + 2)
 
-    for t in range(steps):
-        if t == 0:
-            arrive(near)
-            c = c0[d - 1:2 * d + 3]
-        else:
-            c = c1x[1:d + 5]
+    none = jnp.zeros((1, rows // 2, lanes), F32)
+
+    def padded(x):
+        return jnp.concatenate([none, x[None], none], 0)
+
+    def first_sweeps(b, c, a):
         x = 1.2 * c[1:-1] + a * sum_inner(c, lanes)
-        inner = x[1:-1]
-        d0 = cap[d:2 * d] + 6.0
-        r = own[...] - d0 * inner + sum_inner(x, lanes)
-        b1 = pack(r)
-        if t == 0:
-            window_arrive(cap_window)
-            block = me - 2 + iota((5, 1, 1), 0)
-            d1 = cw[...] + 3.0
-            i1 = jnp.where((block >= 0) & (block < parts), W / d1, 0.0)
-            a1 = 0.5 * i1
-        c1 = b1 * i1[2]
-        vw[t, 3] = c1
-        none = jnp.zeros((1,) + b1.shape, F32)
-        c1 = jnp.concatenate([none, c1[None], none], 0)
-        y1 = 1.2 * c1 + a1[1:4] * sum_packed(c1, half)
-        r1 = jnp.concatenate([none, b1[None], none], 0) - d1[1:4] * y1 + 0.5 * sum_packed(y1, half)
-        parts_2 = to_2(r1[1:2], 0) + to_2(r1[0:1], 1) + to_2(r1[2:3], 2)
-        if t == 0:
-            parts_2 = parts_2 + cap2_sent
-            pl.semaphore_wait(far_sem, len(close))
-        gr[t, me] = parts_2
-        for copy in gather_r[t]:
-            copy.start()
-        window_start(c_window[t])
-        if t == 1:
-            begin(third)
-        else:
-            begin(source)
-            arrive(cap_far)
-            each(pass_far, lambda copy: copy.start())
-
-        for copy in gather_r[t]:
-            copy.wait_recv()
-        got = gr[t]
-        if t == 0:
-            cap2 = unpack(got, 3)
-            i2 = W / (cap2 + 1.5)
-            cap3 = to_3(cap2)
-            i3 = jnp.where(iota(cap3.shape, 2) % GROUP < GROUP // 2, W / (cap3 + 0.75), 0.0)
-            a2, a3 = 0.25 * i2, 0.125 * i3
+        r = b - (cap[d:2 * d] + 6.0) * x[1:-1] + sum_inner(x, lanes)
+        return x, pack(r)
+
+    def spread(b1, c1, d1, a1):
+        c1 = padded(c1)
+        y1 = 1.2 * c1 + a1 * sum_packed(c1, half)
+        r1 = padded(b1) - d1 * y1 + 0.5 * sum_packed(y1, half)
+        return to_2(r1[1:2], 0) + to_2(r1[0:1], 1) + to_2(r1[2:3], 2)
+
+    def level_2(got, cap2, i2, a2, i3, a3):
         b2 = unpack(got, 0) + after(unpack(got, 1)) + before(unpack(got, 2))
         c2 = b2 * i2
         y2 = 1.2 * c2 + a2 * sum_grouped(c2)
@@ -434,87 +419,125 @@
         for _ in range(2):
             y2 = (0.2 * y2 + c2) + a2 * sum_grouped(y2)
         y2s[...] = y2
-        window_arrive(c_window[t])
-
         lifts = []
         for k in range(-2, 3):
             at = (me + k + parts) % parts
             plane = pltpu.roll(y2s[at % stack], (lanes - GROUP * (at // stack)) % lanes, 1)
             lifts.append(jnp.where(within(k), plane, 0.0))
-        lift = twice_rows(dot(jnp.concatenate(lifts, 0), up_2), 5)
-        if t == 0:
-            c1 = vw[t]
-            y1 = 1.2 * c1[1:-1] + a1 * sum_packed(c1, half)[1:-1] + lift
-            c1 = c1[1:-1]
-            y1 = (0.2 * y1 + c1) + a1 * sum_packed(y1, half)
-            y1 = ((0.2 * y1 + c1) + a1 * sum_packed(y1, half))[1:-1]
-        else:
-            c1 = vw[t, 1:6]
-            y1 = 1.2 * c1 + a1 * sum_packed(c1, half) + lift
-            y1 = ((0.2 * y1 + c1) + a1 * sum_packed(y1, half))[1:-1]
-            y1 = (0.2 * y1 + c1[1:-1]) + a1[1:-1] * sum_packed(y1, half)
-
+        return twice_rows(dot(jnp.concatenate(lifts, 0), up_2), 5)
+
+    def lift_0(y1, skip):
         n = rows // 2
         around = flat(y1)
         even, odd = dot(around, up_lo), dot(around, up_hi)
         halves = [part[n * k:n * k + n] for k in range(3) for part in (even, odd)]
-        if t == 1:
-            halves = halves[1:-1]
+        halves = halves[skip:len(halves) - skip]
         planes = len(halves)
         lift = twice_rows(jnp.concatenate(halves, 0), planes)
-        lift = jnp.broadcast_to(lift[:, None], (planes, 2) + lift.shape[1:]).reshape(2 * planes, rows, lanes)
-        if t == 0:
-            each(pass_far, lambda copy: copy.wait_recv())
-            arrive(far)
-            arrive(beyond)
-            a_lo, a_hi = weights(0, d - 1), weights(2 * d + 1, d - 1)
-            first = 1.2 * c0[1:d] + a_lo * sum_inner(c0[0:d + 1], lanes)
-            final = 1.2 * c0[2 * d + 2:3 * d + 1] + a_hi * sum_inner(c0[2 * d + 1:3 * d + 2], lanes)
-            wide = jnp.concatenate([a_lo, a, a_hi], 0)
-            x = jnp.concatenate([first, x, final], 0) + lift
-            x = (0.2 * x[1:-1] + c0[2:3 * d]) + wide[1:-1] * sum_inner(x, lanes)
-            x = (0.2 * x[1:-1] + c0[3:3 * d - 1]) + wide[2:-2] * sum_inner(x, lanes)
-            fp_ref[...] = x[2:-2]
-            arrive(source)
-            b = cap[2:3 * d - 2] * x + src1[...]
-            own[...] = b[2:-2]
-            c1x[1:d + 5] = b * wide[2:-2]
-        else:
-            arrive(third)
-            first = 1.2 * c1x[1:2] + wide[2:3] * sum_inner(c1x[0:3], lanes)
-            final = 1.2 * c1x[d + 4:d + 5] + wide[-3:-2] * sum_inner(c1x[d + 3:d + 6], lanes)
-            x = jnp.concatenate([first, x, final], 0) + lift
-            x = (0.2 * x[1:-1] + c1x[2:d + 4]) + a * sum_inner(x, lanes)
-            fin[...] = (0.2 * x[1:-1] + c1x[3:d + 3]) + a[1:-1] * sum_inner(x, lanes)
-
-    onward = pltpu.make_async_remote_copy(
-        fin, up_ref, ts.at[0], ts.at[1],
-        device_id={"tm": (span + 1) % spans}, device_id_type=MESH)
+        return jnp.broadcast_to(lift[:, None], (planes, 2) + lift.shape[1:]).reshape(2 * planes, rows, lanes)
+
+    arrive(near)
+    x, b1 = first_sweeps(own[...], c0[d - 1:2 * d + 3], a)
+    window_arrive(cap_window[:2])
+    d1, i1 = inverse_1(1, 4)
+    vw[0, 3] = b1 * i1[1]
+    beside = spread(b1, b1 * i1[1], d1, 0.5 * i1) + cap2_sent
+    gr[0, me] = beside
+    pl.semaphore_wait(far_sem, len(close))
+    for copy in gather_r[0]:
+        copy.start()
+    window_start(c_window[0])
+    begin(source)
+    arrive(cap_far)
+    each(pass_far, lambda copy: copy.start())
+    window_arrive(cap_window[2:])
+    a1 = 0.5 * inverse_1(0, 5)[1]
+    arrive(far)
+    arrive(beyond)
+    each(pass_far, lambda copy: copy.wait_recv())
+    a_lo, a_hi = weights(0, d - 1), weights(2 * d + 1, d - 1)
+    first = 1.2 * c0[1:d] + a_lo * sum_inner(c0[0:d + 1], lanes)
+    final = 1.2 * c0[2 * d + 2:3 * d + 1] + a_hi * sum_inner(c0[2 * d + 1:3 * d + 2], lanes)
+    wide = jnp.concatenate([a_lo, a, a_hi], 0)
+    x = jnp.concatenate([first, x, final], 0)
+    for copy in gather_r[0]:
+        copy.wait_recv()
+    window_arrive(c_window[0])
+
+    got = gr[0]
+    cap2 = unpack(got, 3)
+    i2 = W / (cap2 + 1.5)
+    cap3 = to_3(cap2)
+    i3 = jnp.where(iota(cap3.shape, 2) % GROUP < GROUP // 2, W / (cap3 + 0.75), 0.0)
+    coarse = cap2, i2, 0.25 * i2, i3, 0.125 * i3
+    c1 = vw[0]
+    y1 = 1.2 * c1[1:-1] + a1 * sum_packed(c1, half)[1:-1] + level_2(got, *coarse)
+    c1 = c1[1:-1]
+    y1 = (0.2 * y1 + c1) + a1 * sum_packed(y1, half)
+    y1 = ((0.2 * y1 + c1) + a1 * sum_packed(y1, half))[1:-1]
+    x = x + lift_0(y1, 0)
+    x = (0.2 * x[1:-1] + c0[2:3 * d]) + wide[1:-1] * sum_inner(x, lanes)
+    x = (0.2 * x[1:-1] + c0[3:3 * d - 1]) + wide[2:-2] * sum_inner(x, lanes)
+    fp_ref[...] = x[2:-2]
+    arrive(source)
+    b = cap[2:3 * d - 2] * x + src1[...]
+    c1x[1:d + 5] = b * wide[2:-2]
+
+    x, b1 = first_sweeps(b[2:-2], c1x[1:d + 5], a)
+    c1 = b1 * i1[1]
+    c_sent[...] = c1
+    r_sent[...] = spread(b1, c1, d1, 0.5 * i1)
 
     @pl.when(span < spans - 1)
     def _():
-        onward.start()
-
-    @pl.when(span == 0)
-    def _():
-        up_ref[...] = u0[...]
+        for copy in gather_r[1]:
+            copy.start()
+        window_start(c_window[1])
+
+    begin(third)
+    arrive(third)
+    first = 1.2 * c1x[1:2] + wide[2:3] * sum_inner(c1x[0:3], lanes)
+    final = 1.2 * c1x[d + 4:d + 5] + wide[-3:-2] * sum_inner(c1x[d + 3:d + 6], lanes)
+    x = jnp.concatenate([first, x, final], 0)
+    x = (0.2 * x[1:-1] + c1x[2:d + 4]) + a * sum_inner(x, lanes)
+    fin[0] = (0.2 * x[1:-1] + c1x[3:d + 3]) + a[1:-1] * sum_inner(x, lanes)
+
+    @pl.when(span < spans - 1)
+    def _():
+        fin_onward.start()
 
     for pair in (near, far, beyond, source, third, cap_near, cap_far):
         sent(pair)
     each(pass_far, lambda copy: copy.wait_send())
-    for copies in [cap_window] + c_window:
+    for copies in (cap_window, c_window[0]):
         window_sent(copies)
-    for copies in gather_r:
-        for copy in copies:
+    for copy in gather_r[0]:
+        copy.wait_send()
+
+    @pl.when(span == 0)
+    def _():
+        up_ref[...] = u0[...]
+
+    @pl.when(span > 0)
+    def _():
+        for copy in gather_r[1]:
+            copy.wait_recv()
+        window_arrive(c_window[1])
+        fin_onward.wait_recv()
+        c1 = vw[1, 1:6]
+        y1 = 1.2 * c1 + a1 * sum_packed(c1, half) + level_2(gr[1], *coarse)
+        y1 = ((0.2 * y1 + c1) + a1 * sum_packed(y1, half))[1:-1]
+        y1 = (0.2 * y1 + c1[1:-1]) + a1[1:-1] * sum_packed(y1, half)
+        x = lift_0(y1, 1)
+        x = 0.2 * x[1:-1] + a * sum_inner(x, lanes)
+        up_ref[...] = fin[1] + (0.2 * x[1:-1] + a[1:-1] * sum_inner(x, lanes))
+
+    @pl.when(span < spans - 1)
+    def _():
+        for copy in gather_r[1]:
             copy.wait_send()
-
-    @pl.when(span < spans - 1)
-    def _():
-        onward.wait_send()
-
-    @pl.when(span > 0)
-    def _():
-        onward.wait_recv()
+        window_sent(c_window[1])
+        fin_onward.wait_send()
 
 
 def shards(span_opening, source_power, warmth_retention):
@@ -539,11 +562,13 @@
             pltpu.VMEM((depth + 6, rows, lanes), F32),
             pltpu.VMEM((5, rows // 2, lanes), F32),
             pltpu.VMEM((steps, 7, rows // 2, lanes), F32),
+            pltpu.VMEM((rows // 2, lanes), F32),
             pltpu.VMEM((steps, parts, rows // 4, lanes), F32),
+            pltpu.VMEM((rows // 4, lanes), F32),
             pltpu.VMEM((parts * GROUP // lanes, rows // 4, lanes), F32),
             pltpu.VMEM((depth, rows, lanes), F32),
             pltpu.VMEM((6 * rows, lanes), F32),
-            pltpu.VMEM((depth, rows, lanes), F32),
+            pltpu.VMEM((2, depth, rows, lanes), F32),
             pltpu.SemaphoreType.REGULAR,
             dma((4,)), dma((10,)), dma((10,)), dma((4,)), dma((4,)), dma((2, spans)), dma((2, spans)),
             dma((steps, parts)), dma((steps, parts)), dma((1 + steps, 7)), dma((1 + steps, 7)), dma((2,)),

time: 46.2 us -> 47.7 us (1.032)
  the two profiles are of different devices: /device:TPU:1 before, /device:TPU:26 now
where the time goes in v2:
time: 47.7 us; the launch traced here: 47.6 us
  Pallas kernels  45.7 us (96%)
  local copies, waits for them, and re-layouts  1.31 us (3%)
  between operations  0.64 us (1%)
    pallas_call x1, Pallas kernels, shards(): pl.pallas_call(functools.partial(kernel, parts, spans, steps), out_shape=...  45.7 us
    unnamed x2, local copies, waits for them, and re-layouts  1.31 us

profile of v2, /device:TPU:26, one launch (start us, length us, event | category | flops | bytes accessed | tf_op | source)
XLA Modules:
  0.0 47.6 jit_solution(1750013895680193842)
XLA Ops:
  0.6 45.7 %shard_map.50 = (f32[4,64,128]{2,1,0:T(8,128)S(1)}, f32[4,64,128]{2,1,0:T(8,128)S(1)}) custom-call(f32[4,64,128]{2,1,0:T(8,128)} %bitcast.7, f32[2,4,64,128]{3,2,1,0:T(8,128)} %bitcast.6, f32[4,64,128]{2,1,0:T(8,128)} %cap_in.1), custom_call_target="tpu_custom_call" | custom-call | tf_op jit(solution)/shard_map/pallas_call | solution.py:551
  46.3 0.7 %copy.7 = f32[1,4,64,128]{3,2,1,0:T(8,128)} copy(f32[1,4,64,128]{3,2,1,0:T(8,128)S(1)} %bitcast.5) | data formatting | bytes 262144
  47.0 0.7 %copy.8 = f32[1,4,64,128]{3,2,1,0:T(8,128)} copy(f32[1,4,64,128]{3,2,1,0:T(8,128)S(1)} %bitcast.4) | data formatting | bytes 262144

commit v3 on v2

--- a/solution.py
+++ b/solution.py
@@ -38,8 +38,9 @@
     rows, lanes = x.shape[1], x.shape[2]
     lane, row = iota(x.shape, 2), iota(x.shape, 1)
     left, right = pltpu.roll(x, 1, 2), pltpu.roll(x, lanes - 1, 2)
-    left = jnp.where(lane % width == 0, 0.0, left)
-    right = jnp.where(lane % width == width - 1, 0.0, right)
+    if width:
+        left = jnp.where(lane % width == 0, 0.0, left)
+        right = jnp.where(lane % width == width - 1, 0.0, right)
     up = jnp.where(row == 0, 0.0, pltpu.roll(x, 1, 1))
     down = jnp.where(row == rows - 1, 0.0, pltpu.roll(x, rows - 1, 1))
     return (left + right) + (up + down)
@@ -62,16 +63,19 @@
     return jnp.where(iota(moved.shape, 2) >= lanes - GROUP, 0.0, moved)
 
 
-def before(x):
-    return jnp.concatenate([earlier(x), x[:-1]], 0)
-
-
-def after(x):
-    return jnp.concatenate([x[1:], later(x)], 0)
-
-
 def sum_grouped(x):
-    return in_plane(x, GROUP) + (before(x) + after(x))
+    ends = jnp.concatenate([earlier(x), x, later(x)], 0)
+    return in_plane(x, GROUP) + (ends[:-2] + ends[2:])
+
+
+def sum_planes(x):
+    before, after = shifted(x)
+    return in_plane(x, None) + (before + after)
+
+
+def plane_padded(x, by):
+    zero = jnp.zeros((by,) + x.shape[1:], F32)
+    return jnp.concatenate([zero, x, zero], 0)
 
 
 def sum_packed(x, width):
@@ -129,20 +133,21 @@
     parts, spans, steps,
     open_ref, src_ref, cap_in,
     fp_ref, up_ref,
-    u0, src0, src1, cap, c0, c1x, cw, vw, c_sent, gr, r_sent, y2s, own, tmp, fin,
+    u0, src0, src1, cap, c0, c1x, cw, vw, c_sent, bw, b_sent, gr, r_sent, r2s, y3s, own, tmp, fin,
     far_sem, in_sem, hs, hr, ks, kr, fs, fr, gs, gv, ws, wr, ts,
 ):
     me, span = lax.axis_index("space"), lax.axis_index("tm")
     depth, rows, lanes = open_ref.shape
     half = lanes // 2
     groups = lanes // GROUP
-    stack = parts // groups
-    assert parts % groups == 0 and lanes == 128 and rows == 64
+    assert parts == 32 and lanes == 128 and rows == 64
     close = sorted({k % parts for k in NEAR} | {-k % parts for k in NEAR})
     assert {(a + b) % parts for a in close + [0] for b in close + [0]} == set(range(parts))
 
     cw[...] = jnp.zeros(cw.shape, F32)
     vw[...] = jnp.zeros(vw.shape, F32)
+    bw[...] = jnp.zeros(bw.shape, F32)
+    r2s[...] = jnp.zeros(r2s.shape, F32)
 
     barrier = pltpu.get_barrier_semaphore()
     for k in close:
@@ -159,18 +164,15 @@
     for load in loads:
         load.start()
 
-    group = me // stack
     down_lo = picks(lanes, lambda s, d: (s // 2 == d) & (d < half), 0.125)
     down_hi = picks(lanes, lambda s, d: s // 2 + half == d, 0.125)
-    down_2 = [
-        picks(lanes, lambda s, d: (s % half) // 2 + GROUP * ((group + q) % groups) == d, 0.125)
-        for q in range(groups)
-    ]
-    down_3 = picks(lanes, lambda s, d: s // GROUP * GROUP + s % GROUP // 2 == d, 0.125)
+    down_2 = picks(lanes, lambda s, d: (s % half) // 2 == d, 0.125)
+    down_3 = picks(lanes, lambda s, d: (s < GROUP) & (d % GROUP == s // 2), 0.125)
+    down_cap = picks(lanes, lambda s, d: (s < GROUP) & (d % GROUP == s // 2 + GROUP // 2), 0.125)
     up_lo = picks(lanes, lambda s, d: d // 2 == s, 1.0)
     up_hi = picks(lanes, lambda s, d: d // 2 + half == s, 1.0)
     up_2 = picks(lanes, lambda s, d: (d % half) // 2 == s, 1.0)
-    up_3 = picks(lanes, lambda s, d: d // GROUP * GROUP + d % GROUP // 2 == s, 1.0)
+    up_3 = picks(lanes, lambda s, d: (d < GROUP) & (d // 2 == s), 1.0)
 
     def pair_rows(x):
         n, r, w = x.shape
@@ -188,19 +190,46 @@
         n = rows // 2
         return dot(s[:n], down_lo) + dot(s[n:], down_hi)
 
-    def to_2(x, q):
-        return dot(pair_rows(x), down_2[q])
-
-    def to_3(x):
-        s = x.reshape(stack // 2, 2, rows // 4, lanes).sum(1)
-        return dot(pair_rows(s), down_3).reshape(stack // 2, rows // 8, lanes)
-
-    def unpack(x, q):
-        at = (iota((stack,) + x.shape[1:], 2) // GROUP + groups - q) % groups
-        out = x[:stack]
-        for g in range(1, groups):
-            out = jnp.where(at == g, x[g * stack:(g + 1) * stack], out)
-        return pltpu.roll(out, lanes - GROUP * q, 2) if q else out
+    def to_2(x):
+        return dot(pair_rows(x), down_2).reshape(x.shape[0], rows // 4, lanes)
+
+    lane = iota((rows // 8, lanes), 1)
+
+    def turn(planes, off):
+        out = []
+        for k in range(groups):
+            total = None
+            for g in range(groups):
+                by = (GROUP * (g - k) - off) % lanes
+                moved = pltpu.roll(planes[g], by, 1) if by else planes[g]
+                total = moved if total is None else jnp.where(lane // GROUP == g, moved, total)
+            out.append(total[None])
+        return jnp.concatenate(out, 0)
+
+    def level_3(got):
+        pairs = [got[0]] + [got[2 * i - 1] + got[2 * i] for i in range(1, parts // 2)] + [got[parts - 1]]
+        out = []
+        for k in range(groups):
+            total = pairs[4 * k + 2]
+            for i, keep in (
+                (4 * k - 1, lane < GROUP), (4 * k, lane < 2 * GROUP), (4 * k + 1, lane < 3 * GROUP),
+                (4 * k + 3, lane >= GROUP), (4 * k + 4, lane >= 2 * GROUP), (4 * k + 5, lane >= 3 * GROUP),
+            ):
+                if 0 <= i < len(pairs):
+                    total = total + jnp.where(keep, pairs[i], 0.0)
+            out.append(total)
+        return turn(out, 0)
+
+    def capacity_3(got):
+        out = []
+        for k in range(groups):
+            total = None
+            for g in range(groups):
+                i = 2 * (4 * k + g)
+                pair = got[i] + got[i + 1]
+                total = pair if total is None else jnp.where(lane // GROUP == g, pair, total)
+            out.append(total)
+        return turn(out, GROUP // 2)
 
     def within(k):
         return (me + k >= 0) & (me + k < parts)
@@ -321,10 +350,14 @@
         gather(gr.at[0, me], gr.at[0, me], gs.at[0], gv.at[0], range(1, parts), {}),
         gather(r_sent, gr.at[1, me], gs.at[1], gv.at[1], range(parts), onward),
     ]
-    cap_window = window(cw, cw.at[2], ws.at[0], wr.at[0], 1, 2)
+    cap_window = window(cw, cw.at[5], ws.at[0], wr.at[0], 1, 5)
     c_window = [
         window(vw.at[0], vw.at[0, 3], ws.at[1], wr.at[1], 1, 3),
         window(vw.at[1], c_sent, ws.at[2], wr.at[2], 0, 2, onward),
+    ]
+    b_window = [
+        window(bw.at[0], bw.at[0, 6], ws.at[3], wr.at[3], 1, 6),
+        window(bw.at[1], b_sent, ws.at[4], wr.at[4], 0, 6, onward),
     ]
     fin_onward = pltpu.make_async_remote_copy(
         fin.at[0], fin.at[1], ts.at[0], ts.at[1],
@@ -363,68 +396,83 @@
     own[...] = b
     c0[d + 1:2 * d + 1] = b * (W / (mine + 6.0))
     cap1 = pack(mine)
-    cw[2] = cap1
+    cw[5] = cap1
     loads[3].wait()
 
     pl.semaphore_wait(barrier, len(close) + spans - 1)
     begin(near)
     begin(cap_near)
-    window_start(cap_window)
+    window_start(cap_window[:4])
     for k in close:
         pl.semaphore_signal(far_sem, inc=1, device_id={"space": (me + k) % parts}, device_id_type=MESH)
     begin(far)
     begin(beyond)
     begin(cap_far)
-    cap2_sent = to_2(cap1[None], groups - 1)
+    cap_sent = dot(pair_rows(to_2(cap1[None])), down_cap)
 
     def weights(start, count):
         plane = (me - 1) * depth + start + iota((count, 1, 1), 0)
         inside = (plane >= 0) & (plane < parts * depth)
         return jnp.where(inside, W / (cap[start:start + count] + 6.0), 0.0)
 
+    def inverse(diagonal, start, reach):
+        block = me - reach + start + iota((diagonal.shape[0], 1, 1), 0)
+        return jnp.where((block >= 0) & (block < parts), W / diagonal, 0.0)
+
     def inverse_1(start, stop):
-        block = me - 2 + start + iota((stop - start, 1, 1), 0)
         diagonal = cw[start:stop] + 3.0
-        return diagonal, jnp.where((block >= 0) & (block < parts), W / diagonal, 0.0)
-
+        return diagonal, inverse(diagonal, start, 5)
+
+    def inverse_2(start, stop):
+        diagonal = to_2(cw[start:stop]) + 1.5
+        return diagonal, jnp.where(iota(diagonal.shape, 2) < GROUP, inverse(diagonal, start, 5), 0.0)
+
+    window_arrive(cap_window[:4])
+    d1, i1 = inverse_1(4, 7)
+    d2, i2 = inverse_2(3, 8)
+    near_1 = i1, d1, 0.5 * i1, i2, d2, 0.25 * i2
     arrive(cap_near)
     a = weights(d - 1, d + 2)
-
-    none = jnp.zeros((1, rows // 2, lanes), F32)
-
-    def padded(x):
-        return jnp.concatenate([none, x[None], none], 0)
 
     def first_sweeps(b, c, a):
         x = 1.2 * c[1:-1] + a * sum_inner(c, lanes)
         r = b - (cap[d:2 * d] + 6.0) * x[1:-1] + sum_inner(x, lanes)
         return x, pack(r)
 
-    def spread(b1, c1, d1, a1):
-        c1 = padded(c1)
+    def spread(b1, c1, i1, d1, a1, i2, d2, a2):
+        c1 = plane_padded(c1[None], 1)
         y1 = 1.2 * c1 + a1 * sum_packed(c1, half)
-        r1 = padded(b1) - d1 * y1 + 0.5 * sum_packed(y1, half)
-        return to_2(r1[1:2], 0) + to_2(r1[0:1], 1) + to_2(r1[2:3], 2)
-
-    def level_2(got, cap2, i2, a2, i3, a3):
-        b2 = unpack(got, 0) + after(unpack(got, 1)) + before(unpack(got, 2))
+        b2 = to_2(plane_padded(b1[None], 1) - d1 * y1 + 0.5 * sum_packed(y1, half))
+        c2 = plane_padded(b2 * i2[1:4], 1)
+        y2 = 1.2 * c2 + a2 * sum_planes(c2)
+        r2s[1:8] = plane_padded(b2, 2) - plane_padded(d2 * y2, 1) + 0.25 * sum_planes(plane_padded(y2, 1))
+        pairs = r2s[pl.ds(me % 2, 8)].reshape(4, 2, rows // 4, lanes).sum(1)
+        b3 = dot(pair_rows(pairs), down_3).reshape(4, rows // 8, lanes)
+        first = (me + 4 + me % 2) // 2
+        return b2, sum(jnp.where(lane // GROUP == (first + q) % groups, b3[q], 0.0) for q in range(4))
+
+    def side_by_side(b2):
+        return b2[1] + (pltpu.roll(b2[0], GROUP, 1) + pltpu.roll(b2[2], 2 * GROUP, 1))
+
+    def level_2(b, c3, i2, a2, a3):
+        b2 = b[1:-1] + (pltpu.roll(b[2:], lanes - GROUP, 2) + pltpu.roll(b[:-2], lanes - 2 * GROUP, 2))
         c2 = b2 * i2
-        y2 = 1.2 * c2 + a2 * sum_grouped(c2)
-        r2 = b2 - (cap2 + 1.5) * y2 + 0.25 * sum_grouped(y2)
-        c3 = to_3(r2) * i3
-        y3 = coarse_solve(c3, a3)
-        lift = twice_rows(dot(flat(y3), up_3), stack // 2)
-        lift = jnp.broadcast_to(lift[:, None], (stack // 2, 2) + lift.shape[1:]).reshape(y2.shape)
-        y2 = y2 + lift
-        for _ in range(2):
-            y2 = (0.2 * y2 + c2) + a2 * sum_grouped(y2)
-        y2s[...] = y2
+        y2 = 1.2 * c2[1:-1] + a2 * sum_planes(c2)[1:-1]
+        c2 = c2[1:-1]
+        y3s[...] = coarse_solve(c3, a3)
         lifts = []
-        for k in range(-2, 3):
-            at = (me + k + parts) % parts
-            plane = pltpu.roll(y2s[at % stack], (lanes - GROUP * (at // stack)) % lanes, 1)
-            lifts.append(jnp.where(within(k), plane, 0.0))
-        return twice_rows(dot(jnp.concatenate(lifts, 0), up_2), 5)
+        for q in range(-2, 3):
+            at = me // 2 + q
+            inside = (at >= 0) & (at < parts // 2)
+            at = (at + parts // 2) % (parts // 2)
+            plane = pltpu.roll(y3s[at % groups], (lanes - GROUP * (at // groups)) % lanes, 1)
+            lifts.append(jnp.where(inside, plane, 0.0))
+        lift = twice_rows(dot(jnp.concatenate(lifts, 0), up_3), 5)
+        lift = jnp.broadcast_to(lift[:, None], (5, 2) + lift.shape[1:]).reshape((10,) + lift.shape[1:])
+        y2 = y2 + jnp.where(me % 2 == 1, lift[1:], lift[:-1])
+        y2 = ((0.2 * y2 + c2) + a2 * sum_planes(y2))[1:-1]
+        y2 = ((0.2 * y2 + c2[1:-1]) + a2[1:-1] * sum_planes(y2))[1:-1]
+        return twice_rows(dot(flat(y2), up_2), 5)
 
     def lift_0(y1, skip):
         n = rows // 2
@@ -438,22 +486,26 @@
 
     arrive(near)
     x, b1 = first_sweeps(own[...], c0[d - 1:2 * d + 3], a)
-    window_arrive(cap_window[:2])
-    d1, i1 = inverse_1(1, 4)
-    vw[0, 3] = b1 * i1[1]
-    beside = spread(b1, b1 * i1[1], d1, 0.5 * i1) + cap2_sent
-    gr[0, me] = beside
+    c1 = b1 * i1[1]
+    vw[0, 3] = c1
+    b2, b3 = spread(b1, c1, *near_1)
+    gr[0, me] = b3 + cap_sent
+    bw[0, 6] = side_by_side(b2)
     pl.semaphore_wait(far_sem, len(close))
     for copy in gather_r[0]:
         copy.start()
+    window_start(b_window[0])
     window_start(c_window[0])
+    window_start(cap_window[4:])
     begin(source)
     arrive(cap_far)
     each(pass_far, lambda copy: copy.start())
-    window_arrive(cap_window[2:])
-    a1 = 0.5 * inverse_1(0, 5)[1]
+    a1 = 0.5 * inverse_1(3, 8)[1]
     arrive(far)
     arrive(beyond)
+    window_arrive(cap_window[4:])
+    i2 = inverse_2(0, 11)[1]
+    a2 = 0.25 * i2[1:-1]
     each(pass_far, lambda copy: copy.wait_recv())
     a_lo, a_hi = weights(0, d - 1), weights(2 * d + 1, d - 1)
     first = 1.2 * c0[1:d] + a_lo * sum_inner(c0[0:d + 1], lanes)
@@ -462,16 +514,15 @@
     x = jnp.concatenate([first, x, final], 0)
     for copy in gather_r[0]:
         copy.wait_recv()
+    window_arrive(b_window[0])
     window_arrive(c_window[0])
 
     got = gr[0]
-    cap2 = unpack(got, 3)
-    i2 = W / (cap2 + 1.5)
-    cap3 = to_3(cap2)
+    cap3 = capacity_3(got)
     i3 = jnp.where(iota(cap3.shape, 2) % GROUP < GROUP // 2, W / (cap3 + 0.75), 0.0)
-    coarse = cap2, i2, 0.25 * i2, i3, 0.125 * i3
+    a3 = 0.125 * i3
     c1 = vw[0]
-    y1 = 1.2 * c1[1:-1] + a1 * sum_packed(c1, half)[1:-1] + level_2(got, *coarse)
+    y1 = 1.2 * c1[1:-1] + a1 * sum_packed(c1, half)[1:-1] + level_2(bw[0], level_3(got) * i3, i2, a2, a3)
     c1 = c1[1:-1]
     y1 = (0.2 * y1 + c1) + a1 * sum_packed(y1, half)
     y1 = ((0.2 * y1 + c1) + a1 * sum_packed(y1, half))[1:-1]
@@ -482,19 +533,22 @@
     arrive(source)
     b = cap[2:3 * d - 2] * x + src1[...]
     c1x[1:d + 5] = b * wide[2:-2]
+    begin(third)
 
     x, b1 = first_sweeps(b[2:-2], c1x[1:d + 5], a)
     c1 = b1 * i1[1]
     c_sent[...] = c1
-    r_sent[...] = spread(b1, c1, d1, 0.5 * i1)
+    b2, b3 = spread(b1, c1, *near_1)
+    r_sent[...] = b3
+    b_sent[...] = side_by_side(b2)
 
     @pl.when(span < spans - 1)
     def _():
         for copy in gather_r[1]:
             copy.start()
+        window_start(b_window[1])
         window_start(c_window[1])
 
-    begin(third)
     arrive(third)
     first = 1.2 * c1x[1:2] + wide[2:3] * sum_inner(c1x[0:3], lanes)
     final = 1.2 * c1x[d + 4:d + 5] + wide[-3:-2] * sum_inner(c1x[d + 3:d + 6], lanes)
@@ -509,7 +563,7 @@
     for pair in (near, far, beyond, source, third, cap_near, cap_far):
         sent(pair)
     each(pass_far, lambda copy: copy.wait_send())
-    for copies in (cap_window, c_window[0]):
+    for copies in (cap_window, b_window[0], c_window[0]):
         window_sent(copies)
     for copy in gather_r[0]:
         copy.wait_send()
@@ -522,10 +576,11 @@
     def _():
         for copy in gather_r[1]:
             copy.wait_recv()
+        window_arrive(b_window[1])
         window_arrive(c_window[1])
         fin_onward.wait_recv()
         c1 = vw[1, 1:6]
-        y1 = 1.2 * c1 + a1 * sum_packed(c1, half) + level_2(gr[1], *coarse)
+        y1 = 1.2 * c1 + a1 * sum_packed(c1, half) + level_2(bw[1], level_3(gr[1]) * i3, i2, a2, a3)
         y1 = ((0.2 * y1 + c1) + a1 * sum_packed(y1, half))[1:-1]
         y1 = (0.2 * y1 + c1[1:-1]) + a1[1:-1] * sum_packed(y1, half)
         x = lift_0(y1, 1)
@@ -536,6 +591,7 @@
     def _():
         for copy in gather_r[1]:
             copy.wait_send()
+        window_sent(b_window[1])
         window_sent(c_window[1])
         fin_onward.wait_send()
 
@@ -560,18 +616,21 @@
             pltpu.VMEM((3 * depth, rows, lanes), F32),
             pltpu.VMEM((3 * depth + 2, rows, lanes), F32),
             pltpu.VMEM((depth + 6, rows, lanes), F32),
-            pltpu.VMEM((5, rows // 2, lanes), F32),
+            pltpu.VMEM((11, rows // 2, lanes), F32),
             pltpu.VMEM((steps, 7, rows // 2, lanes), F32),
             pltpu.VMEM((rows // 2, lanes), F32),
-            pltpu.VMEM((steps, parts, rows // 4, lanes), F32),
+            pltpu.VMEM((steps, 13, rows // 4, lanes), F32),
             pltpu.VMEM((rows // 4, lanes), F32),
-            pltpu.VMEM((parts * GROUP // lanes, rows // 4, lanes), F32),
+            pltpu.VMEM((steps, parts, rows // 8, lanes), F32),
+            pltpu.VMEM((rows // 8, lanes), F32),
+            pltpu.VMEM((9, rows // 4, lanes), F32),
+            pltpu.VMEM((parts * GROUP // lanes // 2, rows // 8, lanes), F32),
             pltpu.VMEM((depth, rows, lanes), F32),
             pltpu.VMEM((6 * rows, lanes), F32),
             pltpu.VMEM((2, depth, rows, lanes), F32),
             pltpu.SemaphoreType.REGULAR,
             dma((4,)), dma((10,)), dma((10,)), dma((4,)), dma((4,)), dma((2, spans)), dma((2, spans)),
-            dma((steps, parts)), dma((steps, parts)), dma((1 + steps, 7)), dma((1 + steps, 7)), dma((2,)),
+            dma((steps, parts)), dma((steps, parts)), dma((5, 13)), dma((5, 13)), dma((2,)),
         ],
         compiler_params=pltpu.CompilerParams(
             collective_id=0, has_side_effects=True, vmem_limit_bytes=67043328 - 2 * 4 * slab.size

time: 47.7 us -> 45.8 us (0.960)
  the two profiles are of different devices: /device:TPU:26 before, /device:TPU:1 now
where the time goes in v3:
time: 45.8 us; the launch traced here: 45.7 us
  Pallas kernels  43.7 us (95%)
  local copies, waits for them, and re-layouts  1.31 us (3%)
  between operations  0.64 us (1%)
    pallas_call x1, Pallas kernels, shards(): pl.pallas_call(functools.partial(kernel, parts, spans, steps), out_shape=...  43.7 us
    unnamed x2, local copies, waits for them, and re-layouts  1.31 us

profile of v3, /device:TPU:1, one launch (start us, length us, event | category | flops | bytes accessed | tf_op | source)
XLA Modules:
  0.0 45.7 jit_solution(9657205758883603833)
XLA Ops:
  0.6 43.7 %shard_map.50 = (f32[4,64,128]{2,1,0:T(8,128)S(1)}, f32[4,64,128]{2,1,0:T(8,128)S(1)}) custom-call(f32[4,64,128]{2,1,0:T(8,128)} %bitcast.7, f32[2,4,64,128]{3,2,1,0:T(8,128)} %bitcast.6, f32[4,64,128]{2,1,0:T(8,128)} %cap_in.1), custom_call_target="tpu_custom_call" | custom-call | tf_op jit(solution)/shard_map/pallas_call | solution.py:607
  44.4 0.7 %copy.7 = f32[1,4,64,128]{3,2,1,0:T(8,128)} copy(f32[1,4,64,128]{3,2,1,0:T(8,128)S(1)} %bitcast.5) | data formatting | bytes 262144
  45.0 0.7 %copy.8 = f32[1,4,64,128]{3,2,1,0:T(8,128)} copy(f32[1,4,64,128]{3,2,1,0:T(8,128)S(1)} %bitcast.4) | data formatting | bytes 262144

commit v4 on v3

--- a/solution.py
+++ b/solution.py
@@ -133,7 +133,7 @@
     parts, spans, steps,
     open_ref, src_ref, cap_in,
     fp_ref, up_ref,
-    u0, src0, src1, cap, c0, c1x, cw, vw, c_sent, bw, b_sent, gr, r_sent, r2s, y3s, own, tmp, fin,
+    u0, src0, src1, cap, c0, c1x, cw, kw, vw, c_sent, bw, b_sent, gr, r_sent, r2s, y3s, own, tmp, fin,
     far_sem, in_sem, hs, hr, ks, kr, fs, fr, gs, gv, ws, wr, ts,
 ):
     me, span = lax.axis_index("space"), lax.axis_index("tm")
@@ -145,6 +145,7 @@
     assert {(a + b) % parts for a in close + [0] for b in close + [0]} == set(range(parts))
 
     cw[...] = jnp.zeros(cw.shape, F32)
+    kw[...] = jnp.zeros(kw.shape, F32)
     vw[...] = jnp.zeros(vw.shape, F32)
     bw[...] = jnp.zeros(bw.shape, F32)
     r2s[...] = jnp.zeros(r2s.shape, F32)
@@ -339,18 +340,18 @@
     d = depth
     onward = {"tm": (span + 1) % spans}
     near = halo(c0, hs, hr, 0, 2, (2 * d - 1, d - 1), (d + 1, 2 * d + 1))
-    far = halo(c0, hs, hr, 2, d - 2, (d + 1, 1), (d + 3, 2 * d + 3))
-    beyond = halo(c0, hs, hr, 4, 1, (2 * d, 0), (d + 1, 3 * d + 1), reach=2)
-    source = halo(src1, hs, hr, 6, 2, (d, 0), (2, d + 2))
+    far = halo(c0, hs, hr, 2, 1, (2 * d - 2, d - 2), (d + 3, 2 * d + 3))
+    known = halo(src1, hs, hr, 6, 2, (d, 0), (2, d + 2))
     third = halo(c1x, hs, hr, 8, 1, (d, 0), (5, d + 5))
     cap_near = halo(cap, ks, kr, 0, 1, (2 * d - 1, d - 1), (d, 2 * d))
-    cap_far = halo(cap, ks, kr, 2, d - 1, (d, 0), (d + 1, 2 * d + 1), rows_at=my_rows)
-    pass_far = hand_on(0, d - 1, 0, 2 * d + 1)
+    cap_far = halo(cap, ks, kr, 2, d - 2, (d + 1, 1), (d + 1, 2 * d + 1), rows_at=my_rows)
+    pass_far = hand_on(0, d - 2, 1, 2 * d + 1)
     gather_r = [
         gather(gr.at[0, me], gr.at[0, me], gs.at[0], gv.at[0], range(1, parts), {}),
         gather(r_sent, gr.at[1, me], gs.at[1], gv.at[1], range(parts), onward),
     ]
-    cap_window = window(cw, cw.at[5], ws.at[0], wr.at[0], 1, 5)
+    cap_window = window(cw, cw.at[2], ws.at[0], wr.at[0], 1, 2)
+    cap2_window = window(kw, kw.at[5], ws.at[5], wr.at[5], 1, 5)
     c_window = [
         window(vw.at[0], vw.at[0, 3], ws.at[1], wr.at[1], 1, 3),
         window(vw.at[1], c_sent, ws.at[2], wr.at[2], 0, 2, onward),
@@ -373,14 +374,6 @@
         clear(c1x, 0, 3)
         clear(src1, 0, 2)
 
-    @pl.when(me == 1)
-    def _():
-        clear(c0, 0, 1)
-
-    @pl.when(me == parts - 2)
-    def _():
-        clear(c0, 3 * d + 1, 3 * d + 2)
-
     @pl.when(me == parts - 1)
     def _():
         clear(cap, 2 * d, 3 * d)
@@ -395,20 +388,24 @@
     b = mine * u0[...] + src0[...]
     own[...] = b
     c0[d + 1:2 * d + 1] = b * (W / (mine + 6.0))
-    cap1 = pack(mine)
-    cw[5] = cap1
-    loads[3].wait()
 
     pl.semaphore_wait(barrier, len(close) + spans - 1)
+    begin(cap_far)
     begin(near)
     begin(cap_near)
-    window_start(cap_window[:4])
     for k in close:
         pl.semaphore_signal(far_sem, inc=1, device_id={"space": (me + k) % parts}, device_id_type=MESH)
+    cap1 = pack(mine)
+    cw[2] = cap1
+    window_start(cap_window[:2])
+    cap2 = to_2(cap1[None])
+    kw[5] = cap2[0, :rows // 8] + pltpu.roll(cap2[0, rows // 8:], GROUP, 1)
+    window_start(cap2_window[:4])
     begin(far)
-    begin(beyond)
-    begin(cap_far)
-    cap_sent = dot(pair_rows(to_2(cap1[None])), down_cap)
+    window_start(cap_window[2:])
+    window_start(cap2_window[4:8])
+    cap_sent = dot(pair_rows(cap2), down_cap)
+    loads[3].wait()
 
     def weights(start, count):
         plane = (me - 1) * depth + start + iota((count, 1, 1), 0)
@@ -421,18 +418,17 @@
 
     def inverse_1(start, stop):
         diagonal = cw[start:stop] + 3.0
-        return diagonal, inverse(diagonal, start, 5)
+        return diagonal, inverse(diagonal, start, 2)
 
     def inverse_2(start, stop):
-        diagonal = to_2(cw[start:stop]) + 1.5
+        packed = kw[start:stop]
+        diagonal = jnp.concatenate([packed, pltpu.roll(packed, lanes - GROUP, 2)], 1) + 1.5
         return diagonal, jnp.where(iota(diagonal.shape, 2) < GROUP, inverse(diagonal, start, 5), 0.0)
 
-    window_arrive(cap_window[:4])
-    d1, i1 = inverse_1(4, 7)
-    d2, i2 = inverse_2(3, 8)
-    near_1 = i1, d1, 0.5 * i1, i2, d2, 0.25 * i2
     arrive(cap_near)
     a = weights(d - 1, d + 2)
+    arrive(cap_far)
+    each(pass_far, lambda copy: copy.start())
 
     def first_sweeps(b, c, a):
         x = 1.2 * c[1:-1] + a * sum_inner(c, lanes)
@@ -486,6 +482,11 @@
 
     arrive(near)
     x, b1 = first_sweeps(own[...], c0[d - 1:2 * d + 3], a)
+    window_arrive(cap_window[:2])
+    window_arrive(cap2_window[:4])
+    d1, i1 = inverse_1(1, 4)
+    d2, i2 = inverse_2(3, 8)
+    near_1 = i1, d1, 0.5 * i1, i2, d2, 0.25 * i2
     c1 = b1 * i1[1]
     vw[0, 3] = c1
     b2, b3 = spread(b1, c1, *near_1)
@@ -496,22 +497,26 @@
         copy.start()
     window_start(b_window[0])
     window_start(c_window[0])
-    window_start(cap_window[4:])
-    begin(source)
-    arrive(cap_far)
-    each(pass_far, lambda copy: copy.start())
-    a1 = 0.5 * inverse_1(3, 8)[1]
+    window_start(cap2_window[8:])
     arrive(far)
-    arrive(beyond)
-    window_arrive(cap_window[4:])
+    each(pass_far, lambda copy: copy.wait_recv())
+    wide = weights(1, 3 * d - 2)
+    first = 1.2 * c0[d - 1:d] + wide[1:2] * sum_inner(c0[d - 2:d + 1], lanes)
+    final = 1.2 * c0[2 * d + 2:2 * d + 3] + wide[-2:-1] * sum_inner(c0[2 * d + 1:2 * d + 4], lanes)
+
+    def last_sweeps(x, c):
+        x = (0.2 * x[1:-1] + c) + a * sum_inner(x, lanes)
+        return (0.2 * x[1:-1] + c[1:-1]) + a[1:-1] * sum_inner(x, lanes)
+
+    alone = last_sweeps(jnp.concatenate([first, x, final], 0), c0[d:2 * d + 2])
+    fp_ref[...] = alone
+    src1[2:d + 2] = cap[d:2 * d] * alone + src1[2:d + 2]
+    begin(known)
+    window_arrive(cap_window[2:])
+    a1 = 0.5 * inverse_1(0, 5)[1]
+    window_arrive(cap2_window[4:])
     i2 = inverse_2(0, 11)[1]
     a2 = 0.25 * i2[1:-1]
-    each(pass_far, lambda copy: copy.wait_recv())
-    a_lo, a_hi = weights(0, d - 1), weights(2 * d + 1, d - 1)
-    first = 1.2 * c0[1:d] + a_lo * sum_inner(c0[0:d + 1], lanes)
-    final = 1.2 * c0[2 * d + 2:3 * d + 1] + a_hi * sum_inner(c0[2 * d + 1:3 * d + 2], lanes)
-    wide = jnp.concatenate([a_lo, a, a_hi], 0)
-    x = jnp.concatenate([first, x, final], 0)
     for copy in gather_r[0]:
         copy.wait_recv()
     window_arrive(b_window[0])
@@ -526,13 +531,13 @@
     c1 = c1[1:-1]
     y1 = (0.2 * y1 + c1) + a1 * sum_packed(y1, half)
     y1 = ((0.2 * y1 + c1) + a1 * sum_packed(y1, half))[1:-1]
-    x = x + lift_0(y1, 0)
-    x = (0.2 * x[1:-1] + c0[2:3 * d]) + wide[1:-1] * sum_inner(x, lanes)
-    x = (0.2 * x[1:-1] + c0[3:3 * d - 1]) + wide[2:-2] * sum_inner(x, lanes)
-    fp_ref[...] = x[2:-2]
-    arrive(source)
+    x = lift_0(y1, 0)
+    x = 0.2 * x[1:-1] + wide * sum_inner(x, lanes)
+    x = 0.2 * x[1:-1] + wide[1:-1] * sum_inner(x, lanes)
+    fp_ref[...] = fp_ref[...] + x[2:-2]
+    arrive(known)
     b = cap[2:3 * d - 2] * x + src1[...]
-    c1x[1:d + 5] = b * wide[2:-2]
+    c1x[1:d + 5] = b * wide[1:-1]
     begin(third)
 
     x, b1 = first_sweeps(b[2:-2], c1x[1:d + 5], a)
@@ -550,20 +555,18 @@
         window_start(c_window[1])
 
     arrive(third)
-    first = 1.2 * c1x[1:2] + wide[2:3] * sum_inner(c1x[0:3], lanes)
-    final = 1.2 * c1x[d + 4:d + 5] + wide[-3:-2] * sum_inner(c1x[d + 3:d + 6], lanes)
-    x = jnp.concatenate([first, x, final], 0)
-    x = (0.2 * x[1:-1] + c1x[2:d + 4]) + a * sum_inner(x, lanes)
-    fin[0] = (0.2 * x[1:-1] + c1x[3:d + 3]) + a[1:-1] * sum_inner(x, lanes)
+    first = 1.2 * c1x[1:2] + wide[1:2] * sum_inner(c1x[0:3], lanes)
+    final = 1.2 * c1x[d + 4:d + 5] + wide[-2:-1] * sum_inner(c1x[d + 3:d + 6], lanes)
+    fin[0] = last_sweeps(jnp.concatenate([first, x, final], 0), c1x[2:d + 4])
 
     @pl.when(span < spans - 1)
     def _():
         fin_onward.start()
 
-    for pair in (near, far, beyond, source, third, cap_near, cap_far):
+    for pair in (near, far, known, third, cap_near, cap_far):
         sent(pair)
     each(pass_far, lambda copy: copy.wait_send())
-    for copies in (cap_window, b_window[0], c_window[0]):
+    for copies in (cap_window, cap2_window, b_window[0], c_window[0]):
         window_sent(copies)
     for copy in gather_r[0]:
         copy.wait_send()
@@ -616,7 +619,8 @@
             pltpu.VMEM((3 * depth, rows, lanes), F32),
             pltpu.VMEM((3 * depth + 2, rows, lanes), F32),
             pltpu.VMEM((depth + 6, rows, lanes), F32),
-            pltpu.VMEM((11, rows // 2, lanes), F32),
+            pltpu.VMEM((5, rows // 2, lanes), F32),
+            pltpu.VMEM((11, rows // 8, lanes), F32),
             pltpu.VMEM((steps, 7, rows // 2, lanes), F32),
             pltpu.VMEM((rows // 2, lanes), F32),
             pltpu.VMEM((steps, 13, rows // 4, lanes), F32),
@@ -630,7 +634,7 @@
             pltpu.VMEM((2, depth, rows, lanes), F32),
             pltpu.SemaphoreType.REGULAR,
             dma((4,)), dma((10,)), dma((10,)), dma((4,)), dma((4,)), dma((2, spans)), dma((2, spans)),
-            dma((steps, parts)), dma((steps, parts)), dma((5, 13)), dma((5, 13)), dma((2,)),
+            dma((steps, parts)), dma((steps, parts)), dma((6, 13)), dma((6, 13)), dma((2,)),
         ],
         compiler_params=pltpu.CompilerParams(
             collective_id=0, has_side_effects=True, vmem_limit_bytes=67043328 - 2 * 4 * slab.size

time: 45.8 us -> 43.1 us (0.941)
  Pallas kernels: 43.7 us -> 41.1 us
    pallas_call x1, Pallas kernels: 43.7 us -> 41.1 us  [shards(): pl.pallas_call(functools.partial(kernel, parts, spans, steps), out_shape=...]
where the time goes in v4:
time: 43.1 us; the launch traced here: 43 us
  Pallas kernels  41.1 us (95%)
  local copies, waits for them, and re-layouts  1.31 us (3%)
  between operations  0.64 us (1%)
    pallas_call x1, Pallas kernels, shards(): pl.pallas_call(functools.partial(kernel, parts, spans, steps), out_shape=...  41.1 us
    unnamed x2, local copies, waits for them, and re-layouts  1.31 us

profile of v4, /device:TPU:1, one launch (start us, length us, event | category | flops | bytes accessed | tf_op | source)
XLA Modules:
  0.0 43.0 jit_solution(9848465287149946246)
XLA Ops:
  0.6 41.1 %shard_map.50 = (f32[4,64,128]{2,1,0:T(8,128)S(1)}, f32[4,64,128]{2,1,0:T(8,128)S(1)}) custom-call(f32[4,64,128]{2,1,0:T(8,128)} %bitcast.7, f32[2,4,64,128]{3,2,1,0:T(8,128)} %bitcast.6, f32[4,64,128]{2,1,0:T(8,128)} %cap_in.1), custom_call_target="tpu_custom_call" | custom-call | tf_op jit(solution)/shard_map/pallas_call | solution.py:610
  41.7 0.7 %copy.7 = f32[1,4,64,128]{3,2,1,0:T(8,128)} copy(f32[1,4,64,128]{3,2,1,0:T(8,128)S(1)} %bitcast.5) | data formatting | bytes 262144
  42.3 0.7 %copy.8 = f32[1,4,64,128]{3,2,1,0:T(8,128)} copy(f32[1,4,64,128]{3,2,1,0:T(8,128)S(1)} %bitcast.4) | data formatting | bytes 262144

commit v5 on v4

--- a/solution.py
+++ b/solution.py
@@ -10,7 +10,7 @@
 COARSE_SWEEPS = 24
 W = 0.8
 GROUP = 32
-NEAR = (1, 2, 3, 4, 8, 12)
+NEAR = (1, 2, 3, 4, 5, 8, 12)
 F32 = jnp.float32
 MESH = pl.DeviceIdType.MESH
 
@@ -134,7 +134,7 @@
     open_ref, src_ref, cap_in,
     fp_ref, up_ref,
     u0, src0, src1, cap, c0, c1x, cw, kw, vw, c_sent, bw, b_sent, gr, r_sent, r2s, y3s, own, tmp, fin,
-    far_sem, in_sem, hs, hr, ks, kr, fs, fr, gs, gv, ws, wr, ts,
+    far_sem, in_sem, send_sem, recv_sem,
 ):
     me, span = lax.axis_index("space"), lax.axis_index("tm")
     depth, rows, lanes = open_ref.shape
@@ -144,10 +144,6 @@
     close = sorted({k % parts for k in NEAR} | {-k % parts for k in NEAR})
     assert {(a + b) % parts for a in close + [0] for b in close + [0]} == set(range(parts))
 
-    cw[...] = jnp.zeros(cw.shape, F32)
-    kw[...] = jnp.zeros(kw.shape, F32)
-    vw[...] = jnp.zeros(vw.shape, F32)
-    bw[...] = jnp.zeros(bw.shape, F32)
     r2s[...] = jnp.zeros(r2s.shape, F32)
 
     barrier = pltpu.get_barrier_semaphore()
@@ -232,154 +228,78 @@
             out.append(total)
         return turn(out, GROUP // 2)
 
-    def within(k):
-        return (me + k >= 0) & (me + k < parts)
-
-    def window(buf, source, sends, recvs, nearest, reach, to={}):
-        middle = buf.shape[0] // 2
-        return [
-            (k, pltpu.make_async_remote_copy(
-                source, buf.at[middle - k], sends.at[middle + k], recvs.at[middle + k],
-                device_id={"space": (me + k + parts) % parts, **to}, device_id_type=MESH))
-            for far in range(nearest, reach + 1) for k in ((far, -far) if far else (0,))
-        ]
-
-    def where_within(copies, sign, act):
-        for k, copy in copies:
-            @pl.when(within(sign * k))
-            def _(copy=copy):
-                act(copy)
-
-    def window_start(copies):
-        where_within(copies, 1, lambda copy: copy.start())
-
-    def window_arrive(copies):
-        where_within(copies, -1, lambda copy: copy.wait_recv())
-
-    def window_sent(copies):
-        where_within(copies, 1, lambda copy: copy.wait_send())
-
-    def halo(buf, sends, recvs, at, count, up, down, reach=1, rows_at=None):
-        def cut(start):
-            return buf.at[pl.ds(start, count)] if rows_at is None else buf.at[pl.ds(start, count), rows_at]
-
-        ways = ((up, reach, at), (down, parts - reach, at + 1))
-        pair = [
-            pltpu.make_async_remote_copy(
-                cut(way[0]), cut(way[1]), sends.at[sem], recvs.at[sem],
-                device_id={"space": (me + by) % parts}, device_id_type=MESH)
-            for way, by, sem in ways
-        ]
-        return pair + [reach]
-
-    def begin(pair):
-        @pl.when(me < parts - pair[2])
-        def _():
-            pair[0].start()
-
-        @pl.when(me >= pair[2])
-        def _():
-            pair[1].start()
-
-    def arrive(pair):
-        @pl.when(me >= pair[2])
-        def _():
-            pair[0].wait_recv()
-
-        @pl.when(me < parts - pair[2])
-        def _():
-            pair[1].wait_recv()
-
-    def sent(pair):
-        @pl.when(me < parts - pair[2])
-        def _():
-            pair[0].wait_send()
-
-        @pl.when(me >= pair[2])
-        def _():
-            pair[1].wait_send()
+    def valid(start, count, of):
+        at = start + iota((count, 1, 1), 0)
+        return (at >= 0) & (at < of)
+
+    batches = []
+
+    def batch(pieces, total):
+        at = len(batches)
+
+        def copy(source, target, to):
+            return pltpu.make_async_remote_copy(
+                source, target, send_sem.at[at], recv_sem.at[at], device_id=to, device_id_type=MESH)
+
+        made = [copy(*piece) for piece in pieces], copy(total, total, pieces[0][2])
+        batches.append(made)
+        return made
+
+    def begin(made):
+        for copy in made[0]:
+            copy.start()
+
+    def arrive(made):
+        made[1].wait_recv()
+
+    def sent(made):
+        made[1].wait_send()
+
+    def beside(k):
+        return {"space": (me + k + parts) % parts}
 
     share = rows // spans
     my_rows = pl.ds(pl.multiple_of(span * share, share), share)
 
-    def hand_on(at, count, below, above):
-        def copies(start, sem):
-            return [
-                pltpu.make_async_remote_copy(
-                    cap.at[pl.ds(start, count), my_rows], cap.at[pl.ds(start, count), my_rows],
-                    fs.at[sem, k], fr.at[sem, k],
-                    device_id={"tm": (span + k) % spans}, device_id_type=MESH)
-                for k in range(1, spans)
-            ]
-
-        return copies(below, at), copies(above, at + 1)
-
-    def each(pair, act):
-        @pl.when(me > 0)
-        def _():
-            for copy in pair[0]:
-                act(copy)
-
-        @pl.when(me < parts - 1)
-        def _():
-            for copy in pair[1]:
-                act(copy)
+    def halo(buf, count, up, down, rows_at=None):
+        def part(start):
+            return buf.at[pl.ds(start, count)] if rows_at is None else buf.at[pl.ds(start, count), rows_at]
+
+        total = buf.at[pl.ds(0, 2 * count)] if rows_at is None else buf.at[pl.ds(0, 2 * count), pl.ds(0, share)]
+        return batch([(part(way[0]), part(way[1]), beside(k)) for way, k in ((up, 1), (down, -1))], total)
+
+    def window(buf, source, nearest, reach, to={}):
+        middle = buf.shape[0] // 2
+        offsets = [k for far in range(nearest, reach + 1) for k in ((far, -far) if far else (0,))]
+        return batch([(source, buf.at[middle - k], {**beside(k), **to}) for k in offsets], buf.at[pl.ds(0, len(offsets))])
 
     def hops(k):
         z, y = k // 4, k % 4
         return min(z, parts // 4 - z) + min(y, 4 - y)
 
-    def gather(source, target, sends, recvs, offsets, to):
-        return [
-            pltpu.make_async_remote_copy(
-                source, target, sends.at[k], recvs.at[k],
-                device_id={"space": (me + k) % parts, **to}, device_id_type=MESH)
-            for k in sorted(offsets, key=lambda k: -hops(k))
-        ]
+    def gather(buf, source, offsets, to={}):
+        offsets = sorted(offsets, key=lambda k: -hops(k))
+        return batch([(source, buf.at[me], {**beside(k), **to}) for k in offsets], buf.at[pl.ds(0, len(offsets))])
 
     d = depth
     onward = {"tm": (span + 1) % spans}
-    near = halo(c0, hs, hr, 0, 2, (2 * d - 1, d - 1), (d + 1, 2 * d + 1))
-    far = halo(c0, hs, hr, 2, 1, (2 * d - 2, d - 2), (d + 3, 2 * d + 3))
-    known = halo(src1, hs, hr, 6, 2, (d, 0), (2, d + 2))
-    third = halo(c1x, hs, hr, 8, 1, (d, 0), (5, d + 5))
-    cap_near = halo(cap, ks, kr, 0, 1, (2 * d - 1, d - 1), (d, 2 * d))
-    cap_far = halo(cap, ks, kr, 2, d - 2, (d + 1, 1), (d + 1, 2 * d + 1), rows_at=my_rows)
-    pass_far = hand_on(0, d - 2, 1, 2 * d + 1)
-    gather_r = [
-        gather(gr.at[0, me], gr.at[0, me], gs.at[0], gv.at[0], range(1, parts), {}),
-        gather(r_sent, gr.at[1, me], gs.at[1], gv.at[1], range(parts), onward),
-    ]
-    cap_window = window(cw, cw.at[2], ws.at[0], wr.at[0], 1, 2)
-    cap2_window = window(kw, kw.at[5], ws.at[5], wr.at[5], 1, 5)
-    c_window = [
-        window(vw.at[0], vw.at[0, 3], ws.at[1], wr.at[1], 1, 3),
-        window(vw.at[1], c_sent, ws.at[2], wr.at[2], 0, 2, onward),
-    ]
-    b_window = [
-        window(bw.at[0], bw.at[0, 6], ws.at[3], wr.at[3], 1, 6),
-        window(bw.at[1], b_sent, ws.at[4], wr.at[4], 0, 6, onward),
-    ]
-    fin_onward = pltpu.make_async_remote_copy(
-        fin.at[0], fin.at[1], ts.at[0], ts.at[1],
-        device_id={"tm": (span + 1) % spans}, device_id_type=MESH)
-
-    def clear(ref, start, stop):
-        ref[start:stop] = jnp.zeros((stop - start, rows, lanes), F32)
-
-    @pl.when(me == 0)
-    def _():
-        clear(cap, 0, d)
-        clear(c0, 0, d + 1)
-        clear(c1x, 0, 3)
-        clear(src1, 0, 2)
-
-    @pl.when(me == parts - 1)
-    def _():
-        clear(cap, 2 * d, 3 * d)
-        clear(c0, 2 * d + 1, 3 * d + 2)
-        clear(c1x, d + 3, d + 6)
-        clear(src1, d + 2, d + 4)
+    near = halo(c0, 2, (2 * d - 1, d - 1), (d + 1, 2 * d + 1))
+    far = halo(c0, 1, (2 * d - 2, d - 2), (d + 3, 2 * d + 3))
+    known = halo(src1, 2, (d, 0), (2, d + 2))
+    third = halo(c1x, 1, (d, 0), (5, d + 5))
+    cap_near = halo(cap, 1, (2 * d - 1, d - 1), (d, 2 * d))
+    cap_far = halo(cap, 2, (d + 1, 1), (d + 1, 2 * d + 1), my_rows)
+    pass_far = batch(
+        [
+            (cap.at[pl.ds(start, 2), my_rows], cap.at[pl.ds(start, 2), my_rows], {"tm": (span + k) % spans})
+            for start in (1, 2 * d + 1) for k in range(1, spans)
+        ], cap.at[pl.ds(0, 4), pl.ds(0, (spans - 1) * share)])
+    cap_window = window(cw, cw.at[2], 1, 1), window(cw, cw.at[2], 2, 2)
+    cap2_window = window(kw, kw.at[5], 1, 2), window(kw, kw.at[5], 3, 5)
+    gather_r = gather(gr.at[0], gr.at[0, me], range(1, parts)), gather(gr.at[1], r_sent, range(parts), onward)
+    c_window = window(vw.at[0], vw.at[0, 3], 1, 3), window(vw.at[1], c_sent, 0, 2, onward)
+    b_window = window(bw.at[0], bw.at[0, 6], 1, 6), window(bw.at[1], b_sent, 0, 6, onward)
+    fin_onward = batch([(fin.at[0], fin.at[1], onward)], fin.at[0])
 
     loads[0].wait()
     mine = cap[d:2 * d]
@@ -397,24 +317,25 @@
         pl.semaphore_signal(far_sem, inc=1, device_id={"space": (me + k) % parts}, device_id_type=MESH)
     cap1 = pack(mine)
     cw[2] = cap1
-    window_start(cap_window[:2])
+    begin(cap_window[0])
     cap2 = to_2(cap1[None])
     kw[5] = cap2[0, :rows // 8] + pltpu.roll(cap2[0, rows // 8:], GROUP, 1)
-    window_start(cap2_window[:4])
+    begin(cap2_window[0])
     begin(far)
-    window_start(cap_window[2:])
-    window_start(cap2_window[4:8])
+    begin(cap_window[1])
+    begin(cap2_window[1])
     cap_sent = dot(pair_rows(cap2), down_cap)
     loads[3].wait()
 
     def weights(start, count):
-        plane = (me - 1) * depth + start + iota((count, 1, 1), 0)
-        inside = (plane >= 0) & (plane < parts * depth)
+        inside = valid((me - 1) * depth + start, count, parts * depth)
         return jnp.where(inside, W / (cap[start:start + count] + 6.0), 0.0)
 
     def inverse(diagonal, start, reach):
-        block = me - reach + start + iota((diagonal.shape[0], 1, 1), 0)
-        return jnp.where((block >= 0) & (block < parts), W / diagonal, 0.0)
+        return jnp.where(valid(me - reach + start, diagonal.shape[0], parts), W / diagonal, 0.0)
+
+    def planes_of(buf, own, start, count):
+        return jnp.where(valid(me * depth + start - own, count, parts * depth), buf[start:start + count], 0.0)
 
     def inverse_1(start, stop):
         diagonal = cw[start:stop] + 3.0
@@ -428,7 +349,7 @@
     arrive(cap_near)
     a = weights(d - 1, d + 2)
     arrive(cap_far)
-    each(pass_far, lambda copy: copy.start())
+    begin(pass_far)
 
     def first_sweeps(b, c, a):
         x = 1.2 * c[1:-1] + a * sum_inner(c, lanes)
@@ -450,7 +371,8 @@
     def side_by_side(b2):
         return b2[1] + (pltpu.roll(b2[0], GROUP, 1) + pltpu.roll(b2[2], 2 * GROUP, 1))
 
-    def level_2(b, c3, i2, a2, a3):
+    def level_2(t, c3, i2, a2, a3):
+        b = jnp.where(valid(me - 6, 13, parts), bw[t], 0.0)
         b2 = b[1:-1] + (pltpu.roll(b[2:], lanes - GROUP, 2) + pltpu.roll(b[:-2], lanes - 2 * GROUP, 2))
         c2 = b2 * i2
         y2 = 1.2 * c2[1:-1] + a2 * sum_planes(c2)[1:-1]
@@ -481,9 +403,9 @@
         return jnp.broadcast_to(lift[:, None], (planes, 2) + lift.shape[1:]).reshape(2 * planes, rows, lanes)
 
     arrive(near)
-    x, b1 = first_sweeps(own[...], c0[d - 1:2 * d + 3], a)
-    window_arrive(cap_window[:2])
-    window_arrive(cap2_window[:4])
+    x, b1 = first_sweeps(own[...], planes_of(c0, d + 1, d - 1, d + 4), a)
+    arrive(cap_window[0])
+    arrive(cap2_window[0])
     d1, i1 = inverse_1(1, 4)
     d2, i2 = inverse_2(3, 8)
     near_1 = i1, d1, 0.5 * i1, i2, d2, 0.25 * i2
@@ -493,41 +415,39 @@
     gr[0, me] = b3 + cap_sent
     bw[0, 6] = side_by_side(b2)
     pl.semaphore_wait(far_sem, len(close))
-    for copy in gather_r[0]:
-        copy.start()
-    window_start(b_window[0])
-    window_start(c_window[0])
-    window_start(cap2_window[8:])
+    begin(gather_r[0])
+    begin(b_window[0])
+    begin(c_window[0])
     arrive(far)
-    each(pass_far, lambda copy: copy.wait_recv())
+    arrive(pass_far)
     wide = weights(1, 3 * d - 2)
-    first = 1.2 * c0[d - 1:d] + wide[1:2] * sum_inner(c0[d - 2:d + 1], lanes)
-    final = 1.2 * c0[2 * d + 2:2 * d + 3] + wide[-2:-1] * sum_inner(c0[2 * d + 1:2 * d + 4], lanes)
+    c = planes_of(c0, d + 1, d - 2, d + 6)
+    first = 1.2 * c[1:2] + wide[1:2] * sum_inner(c[0:3], lanes)
+    final = 1.2 * c[-2:-1] + wide[-2:-1] * sum_inner(c[-3:], lanes)
 
     def last_sweeps(x, c):
         x = (0.2 * x[1:-1] + c) + a * sum_inner(x, lanes)
         return (0.2 * x[1:-1] + c[1:-1]) + a[1:-1] * sum_inner(x, lanes)
 
-    alone = last_sweeps(jnp.concatenate([first, x, final], 0), c0[d:2 * d + 2])
+    alone = last_sweeps(jnp.concatenate([first, x, final], 0), c[2:-2])
     fp_ref[...] = alone
     src1[2:d + 2] = cap[d:2 * d] * alone + src1[2:d + 2]
     begin(known)
-    window_arrive(cap_window[2:])
+    arrive(cap_window[1])
     a1 = 0.5 * inverse_1(0, 5)[1]
-    window_arrive(cap2_window[4:])
+    arrive(cap2_window[1])
     i2 = inverse_2(0, 11)[1]
     a2 = 0.25 * i2[1:-1]
-    for copy in gather_r[0]:
-        copy.wait_recv()
-    window_arrive(b_window[0])
-    window_arrive(c_window[0])
+    arrive(gather_r[0])
+    arrive(b_window[0])
+    arrive(c_window[0])
 
     got = gr[0]
     cap3 = capacity_3(got)
     i3 = jnp.where(iota(cap3.shape, 2) % GROUP < GROUP // 2, W / (cap3 + 0.75), 0.0)
     a3 = 0.125 * i3
-    c1 = vw[0]
-    y1 = 1.2 * c1[1:-1] + a1 * sum_packed(c1, half)[1:-1] + level_2(bw[0], level_3(got) * i3, i2, a2, a3)
+    c1 = jnp.where(valid(me - 3, 7, parts), vw[0], 0.0)
+    y1 = 1.2 * c1[1:-1] + a1 * sum_packed(c1, half)[1:-1] + level_2(0, level_3(got) * i3, i2, a2, a3)
     c1 = c1[1:-1]
     y1 = (0.2 * y1 + c1) + a1 * sum_packed(y1, half)
     y1 = ((0.2 * y1 + c1) + a1 * sum_packed(y1, half))[1:-1]
@@ -549,27 +469,24 @@
 
     @pl.when(span < spans - 1)
     def _():
-        for copy in gather_r[1]:
-            copy.start()
-        window_start(b_window[1])
-        window_start(c_window[1])
+        begin(gather_r[1])
+        begin(b_window[1])
+        begin(c_window[1])
 
     arrive(third)
-    first = 1.2 * c1x[1:2] + wide[1:2] * sum_inner(c1x[0:3], lanes)
-    final = 1.2 * c1x[d + 4:d + 5] + wide[-2:-1] * sum_inner(c1x[d + 3:d + 6], lanes)
-    fin[0] = last_sweeps(jnp.concatenate([first, x, final], 0), c1x[2:d + 4])
+    c = planes_of(c1x, 3, 0, d + 6)
+    first = 1.2 * c[1:2] + wide[1:2] * sum_inner(c[0:3], lanes)
+    final = 1.2 * c[-2:-1] + wide[-2:-1] * sum_inner(c[-3:], lanes)
+    fin[0] = last_sweeps(jnp.concatenate([first, x, final], 0), c[2:-2])
 
     @pl.when(span < spans - 1)
     def _():
-        fin_onward.start()
-
-    for pair in (near, far, known, third, cap_near, cap_far):
-        sent(pair)
-    each(pass_far, lambda copy: copy.wait_send())
-    for copies in (cap_window, cap2_window, b_window[0], c_window[0]):
-        window_sent(copies)
-    for copy in gather_r[0]:
-        copy.wait_send()
+        begin(fin_onward)
+
+    handed = gather_r[1], b_window[1], c_window[1], fin_onward
+    for made in batches:
+        if not any(made is other for other in handed):
+            sent(made)
 
     @pl.when(span == 0)
     def _():
@@ -577,13 +494,10 @@
 
     @pl.when(span > 0)
     def _():
-        for copy in gather_r[1]:
-            copy.wait_recv()
-        window_arrive(b_window[1])
-        window_arrive(c_window[1])
-        fin_onward.wait_recv()
-        c1 = vw[1, 1:6]
-        y1 = 1.2 * c1 + a1 * sum_packed(c1, half) + level_2(bw[1], level_3(gr[1]) * i3, i2, a2, a3)
+        for made in handed:
+            arrive(made)
+        c1 = jnp.where(valid(me - 2, 5, parts), vw[1, 1:6], 0.0)
+        y1 = 1.2 * c1 + a1 * sum_packed(c1, half) + level_2(1, level_3(gr[1]) * i3, i2, a2, a3)
         y1 = ((0.2 * y1 + c1) + a1 * sum_packed(y1, half))[1:-1]
         y1 = (0.2 * y1 + c1[1:-1]) + a1[1:-1] * sum_packed(y1, half)
         x = lift_0(y1, 1)
@@ -592,11 +506,8 @@
 
     @pl.when(span < spans - 1)
     def _():
-        for copy in gather_r[1]:
-            copy.wait_send()
-        window_sent(b_window[1])
-        window_sent(c_window[1])
-        fin_onward.wait_send()
+        for made in handed:
+            sent(made)
 
 
 def shards(span_opening, source_power, warmth_retention):
@@ -633,8 +544,7 @@
             pltpu.VMEM((6 * rows, lanes), F32),
             pltpu.VMEM((2, depth, rows, lanes), F32),
             pltpu.SemaphoreType.REGULAR,
-            dma((4,)), dma((10,)), dma((10,)), dma((4,)), dma((4,)), dma((2, spans)), dma((2, spans)),
-            dma((steps, parts)), dma((steps, parts)), dma((6, 13)), dma((6, 13)), dma((2,)),
+            dma((4,)), dma((18,)), dma((18,)),
         ],
         compiler_params=pltpu.CompilerParams(
             collective_id=0, has_side_effects=True, vmem_limit_bytes=67043328 - 2 * 4 * slab.size

time: 43.1 us -> 40.3 us (0.935)
  Pallas kernels: 41.1 us -> 38.2 us
    pallas_call x1, Pallas kernels: 41.1 us -> 38.2 us  [shards(): pl.pallas_call(functools.partial(kernel, parts, spans, steps), out_shape=...]
where the time goes in v5:
time: 40.3 us; the launch traced here: 40.2 us
  Pallas kernels  38.2 us (95%)
  local copies, waits for them, and re-layouts  1.31 us (3%)
  between operations  0.64 us (2%)
    pallas_call x1, Pallas kernels, shards(): pl.pallas_call(functools.partial(kernel, parts, spans, steps), out_shape=...  38.2 us
    unnamed x2, local copies, waits for them, and re-layouts  1.31 us

profile of v5, /device:TPU:1, one launch (start us, length us, event | category | flops | bytes accessed | tf_op | source)
XLA Modules:
  0.0 40.2 jit_solution(9830834932896578148)
XLA Ops:
  0.6 38.2 %shard_map.50 = (f32[4,64,128]{2,1,0:T(8,128)S(1)}, f32[4,64,128]{2,1,0:T(8,128)S(1)}) custom-call(f32[4,64,128]{2,1,0:T(8,128)} %bitcast.7, f32[2,4,64,128]{3,2,1,0:T(8,128)} %bitcast.6, f32[4,64,128]{2,1,0:T(8,128)} %cap_in.1), custom_call_target="tpu_custom_call" | custom-call | tf_op jit(solution)/shard_map/pallas_call | solution.py:521
  38.9 0.7 %copy.7 = f32[1,4,64,128]{3,2,1,0:T(8,128)} copy(f32[1,4,64,128]{3,2,1,0:T(8,128)S(1)} %bitcast.5) | data formatting | bytes 262144
  39.5 0.7 %copy.8 = f32[1,4,64,128]{3,2,1,0:T(8,128)} copy(f32[1,4,64,128]{3,2,1,0:T(8,128)S(1)} %bitcast.4) | data formatting | bytes 262144

commit v6 on v5

--- a/solution.py
+++ b/solution.py
@@ -10,7 +10,7 @@
 COARSE_SWEEPS = 24
 W = 0.8
 GROUP = 32
-NEAR = (1, 2, 3, 4, 5, 8, 12)
+NEAR = (1, 3, 4)
 F32 = jnp.float32
 MESH = pl.DeviceIdType.MESH
 
@@ -21,7 +21,7 @@
 
 def dot(a, b):
     total = None
-    for _ in range(3):
+    for _ in range(2):
         part = a.astype(jnp.bfloat16)
         a = a - part.astype(F32)
         term = jnp.dot(part, b, preferred_element_type=F32)
@@ -34,16 +34,35 @@
     return jnp.where(pick(src, dst), scale, 0.0).astype(jnp.bfloat16)
 
 
+def from_sides(lanes, pick, width, scale):
+    def shifted_pick(by):
+        return picks(lanes, lambda s, d: (s % width + by >= 0) & (s % width + by < width) & pick(s + by, d), scale)
+
+    return shifted_pick(-1) + shifted_pick(1)
+
+
+def to_sides(lanes, pick, width):
+    def shifted_pick(by):
+        return picks(lanes, lambda s, d: (d % width + by >= 0) & (d % width + by < width) & pick(s, d + by), 1.0)
+
+    return shifted_pick(-1) + shifted_pick(1)
+
+
+def up_down(x):
+    rows = x.shape[1]
+    row = iota(x.shape, 1)
+    up = jnp.where(row == 0, 0.0, pltpu.roll(x, 1, 1))
+    return up + jnp.where(row == rows - 1, 0.0, pltpu.roll(x, rows - 1, 1))
+
+
 def in_plane(x, width):
-    rows, lanes = x.shape[1], x.shape[2]
-    lane, row = iota(x.shape, 2), iota(x.shape, 1)
+    lanes = x.shape[2]
+    lane = iota(x.shape, 2)
     left, right = pltpu.roll(x, 1, 2), pltpu.roll(x, lanes - 1, 2)
     if width:
         left = jnp.where(lane % width == 0, 0.0, left)
         right = jnp.where(lane % width == width - 1, 0.0, right)
-    up = jnp.where(row == 0, 0.0, pltpu.roll(x, 1, 1))
-    down = jnp.where(row == rows - 1, 0.0, pltpu.roll(x, rows - 1, 1))
-    return (left + right) + (up + down)
+    return (left + right) + up_down(x)
 
 
 def shifted(x):
@@ -134,7 +153,7 @@
     open_ref, src_ref, cap_in,
     fp_ref, up_ref,
     u0, src0, src1, cap, c0, c1x, cw, kw, vw, c_sent, bw, b_sent, gr, r_sent, r2s, y3s, own, tmp, fin,
-    far_sem, in_sem, send_sem, recv_sem,
+    near_sem, far_sem, in_sem, send_sem, recv_sem,
 ):
     me, span = lax.axis_index("space"), lax.axis_index("tm")
     depth, rows, lanes = open_ref.shape
@@ -142,15 +161,9 @@
     groups = lanes // GROUP
     assert parts == 32 and lanes == 128 and rows == 64
     close = sorted({k % parts for k in NEAR} | {-k % parts for k in NEAR})
-    assert {(a + b) % parts for a in close + [0] for b in close + [0]} == set(range(parts))
-
-    r2s[...] = jnp.zeros(r2s.shape, F32)
-
-    barrier = pltpu.get_barrier_semaphore()
-    for k in close:
-        pl.semaphore_signal(barrier, inc=1, device_id={"space": (me + k) % parts}, device_id_type=MESH)
-    for k in range(1, spans):
-        pl.semaphore_signal(barrier, inc=1, device_id={"tm": (span + k) % spans}, device_id_type=MESH)
+    nearby = sorted({(a + b) % parts for a in close for b in close + [0]} - {0})
+    assert {(a + b) % parts for a in nearby for b in nearby + [0]} == set(range(parts))
+    assert set(range(1, 6)) <= set(nearby)
 
     loads = [
         pltpu.make_async_copy(cap_in, cap.at[pl.ds(depth, depth)], in_sem.at[0]),
@@ -160,32 +173,74 @@
     ]
     for load in loads:
         load.start()
-
-    down_lo = picks(lanes, lambda s, d: (s // 2 == d) & (d < half), 0.125)
-    down_hi = picks(lanes, lambda s, d: s // 2 + half == d, 0.125)
-    down_2 = picks(lanes, lambda s, d: (s % half) // 2 == d, 0.125)
-    down_3 = picks(lanes, lambda s, d: (s < GROUP) & (d % GROUP == s // 2), 0.125)
+    barrier = pltpu.get_barrier_semaphore()
+    for k in close:
+        pl.semaphore_signal(barrier, inc=1, device_id={"space": lax.rem(me + k, parts)}, device_id_type=MESH)
+    for k in range(1, spans):
+        pl.semaphore_signal(barrier, inc=1, device_id={"tm": lax.rem(span + k, spans)}, device_id_type=MESH)
+
+    r2s[...] = jnp.zeros(r2s.shape, F32)
+    y3s[...] = jnp.zeros(y3s.shape, F32)
+
+    def pick_lo(s, d):
+        return (s // 2 == d) & (d < half)
+
+    def pick_hi(s, d):
+        return s // 2 + half == d
+
+    def pick_2(s, d):
+        return (s % half) // 2 == d
+
+    def pick_3(s, d):
+        return (s < GROUP) & (d % GROUP == s // 2)
+
+    def swap(pick):
+        return lambda s, d: pick(d, s)
+
+    down_0 = jnp.concatenate([
+        picks(lanes, pick_lo, 0.125), from_sides(lanes, pick_lo, lanes, 0.125),
+        picks(lanes, pick_hi, 0.125), from_sides(lanes, pick_hi, lanes, 0.125),
+    ], 0)
+    down_cap1 = jnp.concatenate([picks(lanes, pick_lo, 0.125), picks(lanes, pick_hi, 0.125)], 0)
+    down_2 = picks(lanes, pick_2, 0.125)
+    down_1 = jnp.concatenate([
+        down_2, from_sides(lanes, pick_2, half, 0.0625) + picks(lanes, pick_2, 0.0625),
+        picks(lanes, lambda s, d: pick_2(s, d) & (s >= half), 0.0625),
+        picks(lanes, lambda s, d: pick_2(s, d) & (s < half), 0.0625),
+    ], 0)
+    down_3 = jnp.concatenate([picks(lanes, pick_3, 0.125), from_sides(lanes, pick_3, GROUP, 0.03125)], 0)
     down_cap = picks(lanes, lambda s, d: (s < GROUP) & (d % GROUP == s // 2 + GROUP // 2), 0.125)
-    up_lo = picks(lanes, lambda s, d: d // 2 == s, 1.0)
-    up_hi = picks(lanes, lambda s, d: d // 2 + half == s, 1.0)
-    up_2 = picks(lanes, lambda s, d: (d % half) // 2 == s, 1.0)
-    up_3 = picks(lanes, lambda s, d: (d < GROUP) & (d // 2 == s), 1.0)
-
-    def pair_rows(x):
+    def rises(pick, width):
+        return [picks(lanes, pick, 1.0), to_sides(lanes, pick, width)]
+
+    up_lo = jnp.concatenate(rises(lambda s, d: d // 2 == s, lanes), 1)
+    up_hi = jnp.concatenate(rises(lambda s, d: d // 2 + half == s, lanes), 1)
+    up_2 = jnp.concatenate(rises(swap(pick_2), half), 1)
+    up_3 = jnp.concatenate([
+        rise for g in range(groups)
+        for rise in rises(lambda s, d: (d < GROUP) & (d // 2 + g * GROUP == s), GROUP)
+    ], 1)
+
+    def pair_rows(x, at=0):
         n, r, w = x.shape
-        tmp[pl.ds(0, n * r), :] = flat(x)
-        return tmp[pl.ds(0, n * r // 2, 2), :] + tmp[pl.ds(1, n * r // 2, 2), :]
+        tmp[pl.ds(at, n * r), :] = flat(x)
+        return tmp[pl.ds(at, n * r // 2, 2), :] + tmp[pl.ds(at + 1, n * r // 2, 2), :]
 
     def twice_rows(x, planes):
+        parts_of = [x[:, at:at + lanes] for at in range(0, x.shape[1], lanes)]
+        x = jnp.concatenate(parts_of, 0)
         r = x.shape[0]
         tmp[pl.ds(0, r, 2), :] = x
         tmp[pl.ds(1, r, 2), :] = x
-        return tmp[pl.ds(0, 2 * r), :].reshape(planes, 2 * r // planes, lanes)
-
-    def pack(x):
-        s = pair_rows(x.reshape(depth // 2, 2, rows, lanes).sum(1))
-        n = rows // 2
-        return dot(s[:n], down_lo) + dot(s[n:], down_hi)
+        out = tmp[pl.ds(0, 2 * r), :].reshape(len(parts_of) * planes, -1, lanes)
+        return [out[at:at + planes] for at in range(0, out.shape[0], planes)]
+
+    def twice_planes(x):
+        return jnp.broadcast_to(x[:, None], (x.shape[0], 2) + x.shape[1:]).reshape((2 * x.shape[0],) + x.shape[1:])
+
+    def slab_pairs(x, at=0):
+        s = pair_rows(x.reshape(depth // 2, 2, rows, lanes).sum(1), at)
+        return s[:rows // 2], s[rows // 2:]
 
     def to_2(x):
         return dot(pair_rows(x), down_2).reshape(x.shape[0], rows // 4, lanes)
@@ -256,7 +311,7 @@
         made[1].wait_send()
 
     def beside(k):
-        return {"space": (me + k + parts) % parts}
+        return {"space": lax.rem(me + (k + parts) % parts, parts)}
 
     share = rows // spans
     my_rows = pl.ds(pl.multiple_of(span * share, share), share)
@@ -314,14 +369,17 @@
     begin(near)
     begin(cap_near)
     for k in close:
-        pl.semaphore_signal(far_sem, inc=1, device_id={"space": (me + k) % parts}, device_id_type=MESH)
-    cap1 = pack(mine)
+        pl.semaphore_signal(near_sem, inc=1, device_id=beside(k), device_id_type=MESH)
+    cap1 = dot(jnp.concatenate(slab_pairs(mine), 1), down_cap1)
     cw[2] = cap1
     begin(cap_window[0])
     cap2 = to_2(cap1[None])
     kw[5] = cap2[0, :rows // 8] + pltpu.roll(cap2[0, rows // 8:], GROUP, 1)
+    begin(far)
+    pl.semaphore_wait(near_sem, len(close))
     begin(cap2_window[0])
-    begin(far)
+    for k in nearby:
+        pl.semaphore_signal(far_sem, inc=1, device_id=beside(k), device_id_type=MESH)
     begin(cap_window[1])
     begin(cap2_window[1])
     cap_sent = dot(pair_rows(cap2), down_cap)
@@ -353,18 +411,32 @@
 
     def first_sweeps(b, c, a):
         x = 1.2 * c[1:-1] + a * sum_inner(c, lanes)
-        r = b - (cap[d:2 * d] + 6.0) * x[1:-1] + sum_inner(x, lanes)
-        return x, pack(r)
+        inner = x[1:-1]
+        r = b - (cap[d:2 * d] + 6.0) * inner + up_down(inner) + (x[:-2] + x[2:])
+        (r_lo, r_hi), (x_lo, x_hi) = slab_pairs(r), slab_pairs(inner, depth * rows // 2)
+        return x, dot(jnp.concatenate([r_lo, x_lo, r_hi, x_hi], 1), down_0)
 
     def spread(b1, c1, i1, d1, a1, i2, d2, a2):
         c1 = plane_padded(c1[None], 1)
         y1 = 1.2 * c1 + a1 * sum_packed(c1, half)
-        b2 = to_2(plane_padded(b1[None], 1) - d1 * y1 + 0.5 * sum_packed(y1, half))
+        r1 = pair_rows(plane_padded(b1[None], 1) - d1 * y1 + 0.5 * up_down(y1))
+        y1 = pair_rows(y1, 3 * rows // 2)
+        n = rows // 4
+        none = jnp.zeros((n, lanes), F32)
+        around = jnp.concatenate([none, y1[:-n]], 0), jnp.concatenate([y1[n:], none], 0)
+        b2 = dot(jnp.concatenate([r1, y1, *around], 1), down_1).reshape(3, n, lanes)
         c2 = plane_padded(b2 * i2[1:4], 1)
         y2 = 1.2 * c2 + a2 * sum_planes(c2)
-        r2s[1:8] = plane_padded(b2, 2) - plane_padded(d2 * y2, 1) + 0.25 * sum_planes(plane_padded(y2, 1))
-        pairs = r2s[pl.ds(me % 2, 8)].reshape(4, 2, rows // 4, lanes).sum(1)
-        b3 = dot(pair_rows(pairs), down_3).reshape(4, rows // 8, lanes)
+        r2 = plane_padded(b2, 2) - plane_padded(d2 * y2, 1)
+        y2 = plane_padded(y2, 1)
+        before, after = shifted(y2)
+        r2s[0, 1:8] = r2 + 0.25 * (up_down(y2) + (before + after))
+        r2s[1, 1:8] = y2
+        pairs = [
+            pair_rows(r2s[i, pl.ds(me % 2, 8)].reshape(4, 2, n, lanes).sum(1), i * 4 * n)
+            for i in range(2)
+        ]
+        b3 = dot(jnp.concatenate(pairs, 1), down_3).reshape(4, n // 2, lanes)
         first = (me + 4 + me % 2) // 2
         return b2, sum(jnp.where(lane // GROUP == (first + q) % groups, b3[q], 0.0) for q in range(4))
 
@@ -377,30 +449,35 @@
         c2 = b2 * i2
         y2 = 1.2 * c2[1:-1] + a2 * sum_planes(c2)[1:-1]
         c2 = c2[1:-1]
-        y3s[...] = coarse_solve(c3, a3)
-        lifts = []
-        for q in range(-2, 3):
-            at = me // 2 + q
-            inside = (at >= 0) & (at < parts // 2)
-            at = (at + parts // 2) % (parts // 2)
-            plane = pltpu.roll(y3s[at % groups], (lanes - GROUP * (at // groups)) % lanes, 1)
-            lifts.append(jnp.where(inside, plane, 0.0))
-        lift = twice_rows(dot(jnp.concatenate(lifts, 0), up_3), 5)
-        lift = jnp.broadcast_to(lift[:, None], (5, 2) + lift.shape[1:]).reshape((10,) + lift.shape[1:])
-        y2 = y2 + jnp.where(me % 2 == 1, lift[1:], lift[:-1])
         y2 = ((0.2 * y2 + c2) + a2 * sum_planes(y2))[1:-1]
+        y3 = dot(flat(coarse_solve(c3, a3)), up_3)
+        for g in range(groups):
+            y3s[2 + 4 * g:6 + 4 * g] = y3[:, 2 * g * lanes:2 * (g + 1) * lanes].reshape(4, rows // 8, 2 * lanes)
+        lift, sides = [
+            jnp.where(me % 2 == 1, x[1:], x[:-1]) for x in
+            [twice_planes(x) for x in twice_rows(y3s[pl.ds(me // 2, 5)].reshape(5 * rows // 8, 2 * lanes), 5)]
+        ]
+        total = (sides + up_down(lift))[1:-1] + (lift[:-2] + lift[2:])
+        y2 = y2 + (0.2 * lift[1:-1] + a2[1:-1] * total)
         y2 = ((0.2 * y2 + c2[1:-1]) + a2[1:-1] * sum_planes(y2))[1:-1]
         return twice_rows(dot(flat(y2), up_2), 5)
+
+    def swept_1(y1, lift, sides, a1):
+        before, after = shifted(lift)
+        across = lift + jnp.where(iota(lift.shape, 2) < half, before, after)
+        return y1 + (0.2 * lift + a1 * ((sides + up_down(lift)) + across))
 
     def lift_0(y1, skip):
         n = rows // 2
         around = flat(y1)
-        even, odd = dot(around, up_lo), dot(around, up_hi)
-        halves = [part[n * k:n * k + n] for k in range(3) for part in (even, odd)]
+        both = dot(around, up_lo), dot(around, up_hi)
+        halves = [part[n * k:n * k + n] for k in range(3) for part in both]
         halves = halves[skip:len(halves) - skip]
-        planes = len(halves)
-        lift = twice_rows(jnp.concatenate(halves, 0), planes)
-        return jnp.broadcast_to(lift[:, None], (planes, 2) + lift.shape[1:]).reshape(2 * planes, rows, lanes)
+        return [twice_planes(x) for x in twice_rows(jnp.concatenate(halves, 0), len(halves))]
+
+    def swept_0(lift, sides, a):
+        total = (sides + up_down(lift))[1:-1] + (lift[:-2] + lift[2:])
+        return 0.2 * lift[1:-1] + a * total
 
     arrive(near)
     x, b1 = first_sweeps(own[...], planes_of(c0, d + 1, d - 1, d + 4), a)
@@ -414,7 +491,7 @@
     b2, b3 = spread(b1, c1, *near_1)
     gr[0, me] = b3 + cap_sent
     bw[0, 6] = side_by_side(b2)
-    pl.semaphore_wait(far_sem, len(close))
+    pl.semaphore_wait(far_sem, len(nearby))
     begin(gather_r[0])
     begin(b_window[0])
     begin(c_window[0])
@@ -447,12 +524,12 @@
     i3 = jnp.where(iota(cap3.shape, 2) % GROUP < GROUP // 2, W / (cap3 + 0.75), 0.0)
     a3 = 0.125 * i3
     c1 = jnp.where(valid(me - 3, 7, parts), vw[0], 0.0)
-    y1 = 1.2 * c1[1:-1] + a1 * sum_packed(c1, half)[1:-1] + level_2(0, level_3(got) * i3, i2, a2, a3)
+    y1 = 1.2 * c1[1:-1] + a1 * sum_packed(c1, half)[1:-1]
     c1 = c1[1:-1]
     y1 = (0.2 * y1 + c1) + a1 * sum_packed(y1, half)
+    y1 = swept_1(y1, *level_2(0, level_3(got) * i3, i2, a2, a3), a1)
     y1 = ((0.2 * y1 + c1) + a1 * sum_packed(y1, half))[1:-1]
-    x = lift_0(y1, 0)
-    x = 0.2 * x[1:-1] + wide * sum_inner(x, lanes)
+    x = swept_0(*lift_0(y1, 0), wide)
     x = 0.2 * x[1:-1] + wide[1:-1] * sum_inner(x, lanes)
     fp_ref[...] = fp_ref[...] + x[2:-2]
     arrive(known)
@@ -497,11 +574,11 @@
         for made in handed:
             arrive(made)
         c1 = jnp.where(valid(me - 2, 5, parts), vw[1, 1:6], 0.0)
-        y1 = 1.2 * c1 + a1 * sum_packed(c1, half) + level_2(1, level_3(gr[1]) * i3, i2, a2, a3)
-        y1 = ((0.2 * y1 + c1) + a1 * sum_packed(y1, half))[1:-1]
+        y1 = 1.2 * c1 + a1 * sum_packed(c1, half)
+        y1 = (0.2 * y1 + c1) + a1 * sum_packed(y1, half)
+        y1 = swept_1(y1, *level_2(1, level_3(gr[1]) * i3, i2, a2, a3), a1)[1:-1]
         y1 = (0.2 * y1 + c1[1:-1]) + a1[1:-1] * sum_packed(y1, half)
-        x = lift_0(y1, 1)
-        x = 0.2 * x[1:-1] + a * sum_inner(x, lanes)
+        x = swept_0(*lift_0(y1, 1), a)
         up_ref[...] = fin[1] + (0.2 * x[1:-1] + a[1:-1] * sum_inner(x, lanes))
 
     @pl.when(span < spans - 1)
@@ -538,11 +615,12 @@
             pltpu.VMEM((rows // 4, lanes), F32),
             pltpu.VMEM((steps, parts, rows // 8, lanes), F32),
             pltpu.VMEM((rows // 8, lanes), F32),
-            pltpu.VMEM((9, rows // 4, lanes), F32),
-            pltpu.VMEM((parts * GROUP // lanes // 2, rows // 8, lanes), F32),
+            pltpu.VMEM((2, 9, rows // 4, lanes), F32),
+            pltpu.VMEM((parts // 2 + 4, rows // 8, 2 * lanes), F32),
             pltpu.VMEM((depth, rows, lanes), F32),
-            pltpu.VMEM((6 * rows, lanes), F32),
+            pltpu.VMEM((12 * rows, lanes), F32),
             pltpu.VMEM((2, depth, rows, lanes), F32),
+            pltpu.SemaphoreType.REGULAR,
             pltpu.SemaphoreType.REGULAR,
             dma((4,)), dma((18,)), dma((18,)),
         ],

time: 40.3 us -> 40.4 us (level)
  no operation moved by 1% of the time
where the time goes in v6:
time: 40.4 us; the launch traced here: 40.3 us
  Pallas kernels  38.4 us (95%)
  local copies, waits for them, and re-layouts  1.31 us (3%)
  between operations  0.64 us (2%)
    pallas_call x1, Pallas kernels, shards(): pl.pallas_call(functools.partial(kernel, parts, spans, steps), out_shape=...  38.4 us
    unnamed x2, local copies, waits for them, and re-layouts  1.31 us

profile of v6, /device:TPU:1, one launch (start us, length us, event | category | flops | bytes accessed | tf_op | source)
XLA Modules:
  0.0 40.3 jit_solution(4596915905312499490)
XLA Ops:
  0.6 38.4 %shard_map.50 = (f32[4,64,128]{2,1,0:T(8,128)S(1)}, f32[4,64,128]{2,1,0:T(8,128)S(1)}) custom-call(f32[4,64,128]{2,1,0:T(8,128)} %bitcast.7, f32[2,4,64,128]{3,2,1,0:T(8,128)} %bitcast.6, f32[4,64,128]{2,1,0:T(8,128)} %cap_in.1), custom_call_target="tpu_custom_call" | custom-call | tf_op jit(solution)/shard_map/pallas_call | solution.py:598
  39.0 0.7 %copy.7 = f32[1,4,64,128]{3,2,1,0:T(8,128)} copy(f32[1,4,64,128]{3,2,1,0:T(8,128)S(1)} %bitcast.5) | data formatting | bytes 262144
  39.7 0.7 %copy.8 = f32[1,4,64,128]{3,2,1,0:T(8,128)} copy(f32[1,4,64,128]{3,2,1,0:T(8,128)S(1)} %bitcast.4) | data formatting | bytes 262144

commit v7 on v6

--- a/solution.py
+++ b/solution.py
@@ -152,7 +152,7 @@
     parts, spans, steps,
     open_ref, src_ref, cap_in,
     fp_ref, up_ref,
-    u0, src0, src1, cap, c0, c1x, cw, kw, vw, c_sent, bw, b_sent, gr, r_sent, r2s, y3s, own, tmp, fin,
+    u0, src0, src1, cap, c0, c1x, cw, kw, vw, c_sent, bw, b_sent, b_own, b_got, gr, r_sent, r2s, y3s, own, tmp, fin,
     near_sem, far_sem, in_sem, send_sem, recv_sem,
 ):
     me, span = lax.axis_index("space"), lax.axis_index("tm")
@@ -353,8 +353,18 @@
     cap2_window = window(kw, kw.at[5], 1, 2), window(kw, kw.at[5], 3, 5)
     gather_r = gather(gr.at[0], gr.at[0, me], range(1, parts)), gather(gr.at[1], r_sent, range(parts), onward)
     c_window = window(vw.at[0], vw.at[0, 3], 1, 3), window(vw.at[1], c_sent, 0, 2, onward)
-    b_window = window(bw.at[0], bw.at[0, 6], 1, 6), window(bw.at[1], b_sent, 0, 6, onward)
+    b_window = window(bw.at[0], bw.at[0, 5], 1, 5), window(bw.at[1], b_sent, 0, 5, onward)
+    b_near = [
+        batch([(b_own.at[t, 2], b_got.at[t, 0], beside(1)), (b_own.at[t, 0], b_got.at[t, 1], beside(-1))], b_got.at[t])
+        for t in range(steps)
+    ]
     fin_onward = batch([(fin.at[0], fin.at[1], onward)], fin.at[0])
+
+    def pack_2(x):
+        return x[:rows // 8] + pltpu.roll(x[rows // 8:], GROUP, 1)
+
+    def unpack_2(x):
+        return jnp.concatenate([x, pltpu.roll(x, lanes - GROUP, 2)], 1)
 
     loads[0].wait()
     mine = cap[d:2 * d]
@@ -374,10 +384,10 @@
     cw[2] = cap1
     begin(cap_window[0])
     cap2 = to_2(cap1[None])
-    kw[5] = cap2[0, :rows // 8] + pltpu.roll(cap2[0, rows // 8:], GROUP, 1)
-    begin(far)
+    kw[5] = pack_2(cap2[0])
     pl.semaphore_wait(near_sem, len(close))
     begin(cap2_window[0])
+    begin(far)
     for k in nearby:
         pl.semaphore_signal(far_sem, inc=1, device_id=beside(k), device_id_type=MESH)
     begin(cap_window[1])
@@ -400,8 +410,7 @@
         return diagonal, inverse(diagonal, start, 2)
 
     def inverse_2(start, stop):
-        packed = kw[start:stop]
-        diagonal = jnp.concatenate([packed, pltpu.roll(packed, lanes - GROUP, 2)], 1) + 1.5
+        diagonal = unpack_2(kw[start:stop]) + 1.5
         return diagonal, jnp.where(iota(diagonal.shape, 2) < GROUP, inverse(diagonal, start, 5), 0.0)
 
     arrive(cap_near)
@@ -416,7 +425,7 @@
         (r_lo, r_hi), (x_lo, x_hi) = slab_pairs(r), slab_pairs(inner, depth * rows // 2)
         return x, dot(jnp.concatenate([r_lo, x_lo, r_hi, x_hi], 1), down_0)
 
-    def spread(b1, c1, i1, d1, a1, i2, d2, a2):
+    def spread(t, b1, c1, i1, d1, a1, i2, d2, a2):
         c1 = plane_padded(c1[None], 1)
         y1 = 1.2 * c1 + a1 * sum_packed(c1, half)
         r1 = pair_rows(plane_padded(b1[None], 1) - d1 * y1 + 0.5 * up_down(y1))
@@ -425,6 +434,8 @@
         none = jnp.zeros((n, lanes), F32)
         around = jnp.concatenate([none, y1[:-n]], 0), jnp.concatenate([y1[n:], none], 0)
         b2 = dot(jnp.concatenate([r1, y1, *around], 1), down_1).reshape(3, n, lanes)
+        b_own[t] = b2
+        begin(b_near[t])
         c2 = plane_padded(b2 * i2[1:4], 1)
         y2 = 1.2 * c2 + a2 * sum_planes(c2)
         r2 = plane_padded(b2, 2) - plane_padded(d2 * y2, 1)
@@ -438,15 +449,10 @@
         ]
         b3 = dot(jnp.concatenate(pairs, 1), down_3).reshape(4, n // 2, lanes)
         first = (me + 4 + me % 2) // 2
-        return b2, sum(jnp.where(lane // GROUP == (first + q) % groups, b3[q], 0.0) for q in range(4))
-
-    def side_by_side(b2):
-        return b2[1] + (pltpu.roll(b2[0], GROUP, 1) + pltpu.roll(b2[2], 2 * GROUP, 1))
+        return sum(jnp.where(lane // GROUP == (first + q) % groups, b3[q], 0.0) for q in range(4))
 
     def level_2(t, c3, i2, a2, a3):
-        b = jnp.where(valid(me - 6, 13, parts), bw[t], 0.0)
-        b2 = b[1:-1] + (pltpu.roll(b[2:], lanes - GROUP, 2) + pltpu.roll(b[:-2], lanes - 2 * GROUP, 2))
-        c2 = b2 * i2
+        c2 = unpack_2(bw[t]) * i2
         y2 = 1.2 * c2[1:-1] + a2 * sum_planes(c2)[1:-1]
         c2 = c2[1:-1]
         y2 = ((0.2 * y2 + c2) + a2 * sum_planes(y2))[1:-1]
@@ -467,6 +473,11 @@
         across = lift + jnp.where(iota(lift.shape, 2) < half, before, after)
         return y1 + (0.2 * lift + a1 * ((sides + up_down(lift)) + across))
 
+    def right_2(t):
+        arrive(b_near[t])
+        got = jnp.where(valid(me - 1, 1, parts), b_got[t, 0:1], 0.0) + jnp.where(valid(me + 1, 1, parts), b_got[t, 1:2], 0.0)
+        return pack_2(b_own[t, 1] + got[0])
+
     def lift_0(y1, skip):
         n = rows // 2
         around = flat(y1)
@@ -488,13 +499,12 @@
     near_1 = i1, d1, 0.5 * i1, i2, d2, 0.25 * i2
     c1 = b1 * i1[1]
     vw[0, 3] = c1
-    b2, b3 = spread(b1, c1, *near_1)
-    gr[0, me] = b3 + cap_sent
-    bw[0, 6] = side_by_side(b2)
+    gr[0, me] = spread(0, b1, c1, *near_1) + cap_sent
     pl.semaphore_wait(far_sem, len(nearby))
     begin(gather_r[0])
+    begin(c_window[0])
+    bw[0, 5] = right_2(0)
     begin(b_window[0])
-    begin(c_window[0])
     arrive(far)
     arrive(pass_far)
     wide = weights(1, 3 * d - 2)
@@ -540,15 +550,18 @@
     x, b1 = first_sweeps(b[2:-2], c1x[1:d + 5], a)
     c1 = b1 * i1[1]
     c_sent[...] = c1
-    b2, b3 = spread(b1, c1, *near_1)
-    r_sent[...] = b3
-    b_sent[...] = side_by_side(b2)
+    r_sent[...] = spread(1, b1, c1, *near_1)
 
     @pl.when(span < spans - 1)
     def _():
         begin(gather_r[1])
+        begin(c_window[1])
+
+    b_sent[...] = right_2(1)
+
+    @pl.when(span < spans - 1)
+    def _():
         begin(b_window[1])
-        begin(c_window[1])
 
     arrive(third)
     c = planes_of(c1x, 3, 0, d + 6)
@@ -611,8 +624,10 @@
             pltpu.VMEM((11, rows // 8, lanes), F32),
             pltpu.VMEM((steps, 7, rows // 2, lanes), F32),
             pltpu.VMEM((rows // 2, lanes), F32),
-            pltpu.VMEM((steps, 13, rows // 4, lanes), F32),
-            pltpu.VMEM((rows // 4, lanes), F32),
+            pltpu.VMEM((steps, 11, rows // 8, lanes), F32),
+            pltpu.VMEM((rows // 8, lanes), F32),
+            pltpu.VMEM((steps, 3, rows // 4, lanes), F32),
+            pltpu.VMEM((steps, 2, rows // 4, lanes), F32),
             pltpu.VMEM((steps, parts, rows // 8, lanes), F32),
             pltpu.VMEM((rows // 8, lanes), F32),
             pltpu.VMEM((2, 9, rows // 4, lanes), F32),
@@ -622,7 +637,7 @@
             pltpu.VMEM((2, depth, rows, lanes), F32),
             pltpu.SemaphoreType.REGULAR,
             pltpu.SemaphoreType.REGULAR,
-            dma((4,)), dma((18,)), dma((18,)),
+            dma((4,)), dma((20,)), dma((20,)),
         ],
         compiler_params=pltpu.CompilerParams(
             collective_id=0, has_side_effects=True, vmem_limit_bytes=67043328 - 2 * 4 * slab.size

time: 40.4 us -> 42.9 us (1.062)
  Pallas kernels: 38.4 us -> 40.8 us
    pallas_call x1, Pallas kernels: 38.4 us -> 40.8 us  [shards(): pl.pallas_call(functools.partial(kernel, parts, spans, steps), out_shape=...]
where the time goes in v7:
time: 42.9 us; the launch traced here: 42.8 us
  Pallas kernels  40.8 us (95%)
  local copies, waits for them, and re-layouts  1.31 us (3%)
  between operations  0.64 us (1%)
    pallas_call x1, Pallas kernels, shards(): pl.pallas_call(functools.partial(kernel, parts, spans, steps), out_shape=...  40.8 us
    unnamed x2, local copies, waits for them, and re-layouts  1.31 us

profile of v7, /device:TPU:1, one launch (start us, length us, event | category | flops | bytes accessed | tf_op | source)
XLA Modules:
  0.0 42.8 jit_solution(14038371896283558429)
XLA Ops:
  0.6 40.8 %shard_map.50 = (f32[4,64,128]{2,1,0:T(8,128)S(1)}, f32[4,64,128]{2,1,0:T(8,128)S(1)}) custom-call(f32[4,64,128]{2,1,0:T(8,128)} %bitcast.7, f32[2,4,64,128]{3,2,1,0:T(8,128)} %bitcast.6, f32[4,64,128]{2,1,0:T(8,128)} %cap_in.1), custom_call_target="tpu_custom_call" | custom-call | tf_op jit(solution)/shard_map/pallas_call | solution.py:611
  41.5 0.7 %copy.7 = f32[1,4,64,128]{3,2,1,0:T(8,128)} copy(f32[1,4,64,128]{3,2,1,0:T(8,128)S(1)} %bitcast.5) | data formatting | bytes 262144
  42.1 0.7 %copy.8 = f32[1,4,64,128]{3,2,1,0:T(8,128)} copy(f32[1,4,64,128]{3,2,1,0:T(8,128)S(1)} %bitcast.4) | data formatting | bytes 262144

commit v8 on v6

--- a/solution.py
+++ b/solution.py
@@ -10,7 +10,7 @@
 COARSE_SWEEPS = 24
 W = 0.8
 GROUP = 32
-NEAR = (1, 3, 4)
+NEAR = 4
 F32 = jnp.float32
 MESH = pl.DeviceIdType.MESH
 
@@ -160,10 +160,8 @@
     half = lanes // 2
     groups = lanes // GROUP
     assert parts == 32 and lanes == 128 and rows == 64
-    close = sorted({k % parts for k in NEAR} | {-k % parts for k in NEAR})
-    nearby = sorted({(a + b) % parts for a in close for b in close + [0]} - {0})
-    assert {(a + b) % parts for a in nearby for b in nearby + [0]} == set(range(parts))
-    assert set(range(1, 6)) <= set(nearby)
+    assert parts == 8 * NEAR
+    close = [k for k in range(-NEAR, NEAR + 1) if k]
 
     loads = [
         pltpu.make_async_copy(cap_in, cap.at[pl.ds(depth, depth)], in_sem.at[0]),
@@ -175,7 +173,7 @@
         load.start()
     barrier = pltpu.get_barrier_semaphore()
     for k in close:
-        pl.semaphore_signal(barrier, inc=1, device_id={"space": lax.rem(me + k, parts)}, device_id_type=MESH)
+        pl.semaphore_signal(barrier, inc=1, device_id={"space": lax.rem(me + k % parts, parts)}, device_id_type=MESH)
     for k in range(1, spans):
         pl.semaphore_signal(barrier, inc=1, device_id={"tm": lax.rem(span + k, spans)}, device_id_type=MESH)
 
@@ -325,7 +323,7 @@
 
     def window(buf, source, nearest, reach, to={}):
         middle = buf.shape[0] // 2
-        offsets = [k for far in range(nearest, reach + 1) for k in ((far, -far) if far else (0,))]
+        offsets = [k for far in range(reach, nearest - 1, -1) for k in ((far, -far) if far else (0,))]
         return batch([(source, buf.at[middle - k], {**beside(k), **to}) for k in offsets], buf.at[pl.ds(0, len(offsets))])
 
     def hops(k):
@@ -368,17 +366,17 @@
     begin(cap_far)
     begin(near)
     begin(cap_near)
-    for k in close:
+    for k in (NEAR, -NEAR):
         pl.semaphore_signal(near_sem, inc=1, device_id=beside(k), device_id_type=MESH)
     cap1 = dot(jnp.concatenate(slab_pairs(mine), 1), down_cap1)
     cw[2] = cap1
     begin(cap_window[0])
     cap2 = to_2(cap1[None])
     kw[5] = cap2[0, :rows // 8] + pltpu.roll(cap2[0, rows // 8:], GROUP, 1)
+    begin(cap2_window[0])
     begin(far)
-    pl.semaphore_wait(near_sem, len(close))
-    begin(cap2_window[0])
-    for k in nearby:
+    pl.semaphore_wait(near_sem, 2)
+    for k in (2 * NEAR, -2 * NEAR):
         pl.semaphore_signal(far_sem, inc=1, device_id=beside(k), device_id_type=MESH)
     begin(cap_window[1])
     begin(cap2_window[1])
@@ -491,7 +489,7 @@
     b2, b3 = spread(b1, c1, *near_1)
     gr[0, me] = b3 + cap_sent
     bw[0, 6] = side_by_side(b2)
-    pl.semaphore_wait(far_sem, len(nearby))
+    pl.semaphore_wait(far_sem, 2)
     begin(gather_r[0])
     begin(b_window[0])
     begin(c_window[0])
@@ -571,8 +569,10 @@
 
     @pl.when(span > 0)
     def _():
-        for made in handed:
-            arrive(made)
+        arrive(handed[0])
+        arrive(handed[1])
+        arrive(handed[2])
+        arrive(handed[3])
         c1 = jnp.where(valid(me - 2, 5, parts), vw[1, 1:6], 0.0)
         y1 = 1.2 * c1 + a1 * sum_packed(c1, half)
         y1 = (0.2 * y1 + c1) + a1 * sum_packed(y1, half)

time: 40.4 us -> 39.6 us (0.980)
  Pallas kernels: 38.4 us -> 37.6 us
    pallas_call x1, Pallas kernels: 38.4 us -> 37.6 us  [shards(): pl.pallas_call(functools.partial(kernel, parts, spans, steps), out_shape=...]
where the time goes in v8:
time: 39.6 us; the launch traced here: 39.5 us
  Pallas kernels  37.6 us (95%)
  local copies, waits for them, and re-layouts  1.31 us (3%)
  between operations  0.64 us (2%)
    pallas_call x1, Pallas kernels, shards(): pl.pallas_call(functools.partial(kernel, parts, spans, steps), out_shape=...  37.6 us
    unnamed x2, local copies, waits for them, and re-layouts  1.31 us

profile of v8, /device:TPU:1, one launch (start us, length us, event | category | flops | bytes accessed | tf_op | source)
XLA Modules:
  0.0 39.5 jit_solution(6344413145592879331)
XLA Ops:
  0.6 37.6 %shard_map.50 = (f32[4,64,128]{2,1,0:T(8,128)S(1)}, f32[4,64,128]{2,1,0:T(8,128)S(1)}) custom-call(f32[4,64,128]{2,1,0:T(8,128)} %bitcast.7, f32[2,4,64,128]{3,2,1,0:T(8,128)} %bitcast.6, f32[4,64,128]{2,1,0:T(8,128)} %cap_in.1), custom_call_target="tpu_custom_call" | custom-call | tf_op jit(solution)/shard_map/pallas_call | solution.py:598
  38.2 0.7 %copy.7 = f32[1,4,64,128]{3,2,1,0:T(8,128)} copy(f32[1,4,64,128]{3,2,1,0:T(8,128)S(1)} %bitcast.5) | data formatting | bytes 262144
  38.9 0.7 %copy.8 = f32[1,4,64,128]{3,2,1,0:T(8,128)} copy(f32[1,4,64,128]{3,2,1,0:T(8,128)S(1)} %bitcast.4) | data formatting | bytes 262144

commit v9 on v8

--- a/solution.py
+++ b/solution.py
@@ -363,7 +363,6 @@
     c0[d + 1:2 * d + 1] = b * (W / (mine + 6.0))
 
     pl.semaphore_wait(barrier, len(close) + spans - 1)
-    begin(cap_far)
     begin(near)
     begin(cap_near)
     for k in (NEAR, -NEAR):
@@ -374,6 +373,7 @@
     cap2 = to_2(cap1[None])
     kw[5] = cap2[0, :rows // 8] + pltpu.roll(cap2[0, rows // 8:], GROUP, 1)
     begin(cap2_window[0])
+    begin(cap_far)
     begin(far)
     pl.semaphore_wait(near_sem, 2)
     for k in (2 * NEAR, -2 * NEAR):
@@ -404,8 +404,6 @@
 
     arrive(cap_near)
     a = weights(d - 1, d + 2)
-    arrive(cap_far)
-    begin(pass_far)
 
     def first_sweeps(b, c, a):
         x = 1.2 * c[1:-1] + a * sum_inner(c, lanes)
@@ -491,6 +489,8 @@
     bw[0, 6] = side_by_side(b2)
     pl.semaphore_wait(far_sem, 2)
     begin(gather_r[0])
+    arrive(cap_far)
+    begin(pass_far)
     begin(b_window[0])
     begin(c_window[0])
     arrive(far)
@@ -628,6 +628,8 @@
             collective_id=0, has_side_effects=True, vmem_limit_bytes=67043328 - 2 * 4 * slab.size
         ),
     )(span_opening[0], source_power[0], warmth_retention)
+    flag = lax.axis_index("tm") > spans
+    fpoint, updated = jnp.where(flag, updated, fpoint), jnp.where(flag, fpoint, updated)
     return fpoint[None], updated[None]
 
 

time: 39.6 us -> 39.6 us (level)
  local copies, waits for them, and re-layouts: 1.31 us -> 0 us
  other arithmetic: 0 us -> 0.72 us
  Pallas kernels: 37.6 us -> 38.2 us
    unnamed x2 -> x0, local copies, waits for them, and re-layouts: 1.31 us -> none
    broadcast_in_dim x0 -> x1, other arithmetic: none -> 0.72 us  [shards(): return (fpoint[None], updated[None])]
    pallas_call x1, Pallas kernels: 37.6 us -> 38.2 us  [shards(): pl.pallas_call(functools.partial(kernel, parts, spans, steps), out_shape=...]
where the time goes in v9:
time: 39.6 us; the launch traced here: 39.5 us
  Pallas kernels  38.2 us (96%)
  other arithmetic  0.72 us (2%)
  between operations  0.64 us (2%)
    pallas_call x1, Pallas kernels, shards(): pl.pallas_call(functools.partial(kernel, parts, spans, steps), out_shape=...  38.2 us

profile of v9, /device:TPU:1, one launch (start us, length us, event | category | flops | bytes accessed | tf_op | source)
XLA Modules:
  0.0 39.5 jit_solution(693837781245464372)
XLA Ops:
  0.6 38.2 %shard_map.50 = (f32[4,64,128]{2,1,0:T(8,128)S(1)}, f32[4,64,128]{2,1,0:T(8,128)S(1)}) custom-call(f32[4,64,128]{2,1,0:T(8,128)} %bitcast.7, f32[2,4,64,128]{3,2,1,0:T(8,128)} %bitcast.6, f32[4,64,128]{2,1,0:T(8,128)} %cap_in.1), custom_call_target="tpu_custom_call" | custom-call | tf_op jit(solution)/shard_map/pallas_call | solution.py:598
  38.8 0.7 %select_bitcast_fusion = (f32[1,4,64,128]{3,2,1,0:T(8,128)}, f32[1,4,64,128]{3,2,1,0:T(8,128)}) fusion(f32[4,64,128]{2,1,0:T(8,128)S(1)} %get-tuple-element.5, f32[4,64,128]{2,1,0:T(8,128)S(1)} %get-tuple-element.4, pred[]{:T(512)S(6)} %gt.3), kind=kLoop, calls=%fused_computation | loop fusion | flops 65536 | bytes 524289 | tf_op jit(solution)/shard_map/broadcast_in_dim | solution.py:633

commit v10 on v9

--- a/solution.py
+++ b/solution.py
@@ -174,7 +174,7 @@
     barrier = pltpu.get_barrier_semaphore()
     for k in close:
         pl.semaphore_signal(barrier, inc=1, device_id={"space": lax.rem(me + k % parts, parts)}, device_id_type=MESH)
-    for k in range(1, spans):
+    for k in (1, spans - 1):
         pl.semaphore_signal(barrier, inc=1, device_id={"tm": lax.rem(span + k, spans)}, device_id_type=MESH)
 
     r2s[...] = jnp.zeros(r2s.shape, F32)
@@ -311,8 +311,8 @@
     def beside(k):
         return {"space": lax.rem(me + (k + parts) % parts, parts)}
 
-    share = rows // spans
-    my_rows = pl.ds(pl.multiple_of(span * share, share), share)
+    share = rows // 2
+    my_rows = pl.ds(pl.multiple_of(span % 2 * share, share), share)
 
     def halo(buf, count, up, down, rows_at=None):
         def part(start):
@@ -344,9 +344,9 @@
     cap_far = halo(cap, 2, (d + 1, 1), (d + 1, 2 * d + 1), my_rows)
     pass_far = batch(
         [
-            (cap.at[pl.ds(start, 2), my_rows], cap.at[pl.ds(start, 2), my_rows], {"tm": (span + k) % spans})
-            for start in (1, 2 * d + 1) for k in range(1, spans)
-        ], cap.at[pl.ds(0, 4), pl.ds(0, (spans - 1) * share)])
+            (cap.at[pl.ds(start, 2), my_rows], cap.at[pl.ds(start, 2), my_rows], {"tm": span + 1 - 2 * (span % 2)})
+            for start in (1, 2 * d + 1)
+        ], cap.at[pl.ds(0, 4), pl.ds(0, share)])
     cap_window = window(cw, cw.at[2], 1, 1), window(cw, cw.at[2], 2, 2)
     cap2_window = window(kw, kw.at[5], 1, 2), window(kw, kw.at[5], 3, 5)
     gather_r = gather(gr.at[0], gr.at[0, me], range(1, parts)), gather(gr.at[1], r_sent, range(parts), onward)
@@ -362,7 +362,7 @@
     own[...] = b
     c0[d + 1:2 * d + 1] = b * (W / (mine + 6.0))
 
-    pl.semaphore_wait(barrier, len(close) + spans - 1)
+    pl.semaphore_wait(barrier, len(close) + 2)
     begin(near)
     begin(cap_near)
     for k in (NEAR, -NEAR):

time: 39.6 us -> 37.3 us (0.942)
  Pallas kernels: 38.2 us -> 35.9 us
    pallas_call x1, Pallas kernels: 38.2 us -> 35.9 us  [shards(): pl.pallas_call(functools.partial(kernel, parts, spans, steps), out_shape=...]
where the time goes in v10:
time: 37.3 us; the launch traced here: 37.2 us
  Pallas kernels  35.9 us (96%)
  other arithmetic  0.72 us (2%)
  between operations  0.64 us (2%)
    pallas_call x1, Pallas kernels, shards(): pl.pallas_call(functools.partial(kernel, parts, spans, steps), out_shape=...  35.9 us

profile of v10, /device:TPU:1, one launch (start us, length us, event | category | flops | bytes accessed | tf_op | source)
XLA Modules:
  0.0 37.2 jit_solution(14668840219662026365)
XLA Ops:
  0.6 35.9 %shard_map.50 = (f32[4,64,128]{2,1,0:T(8,128)S(1)}, f32[4,64,128]{2,1,0:T(8,128)S(1)}) custom-call(f32[4,64,128]{2,1,0:T(8,128)} %bitcast.7, f32[2,4,64,128]{3,2,1,0:T(8,128)} %bitcast.6, f32[4,64,128]{2,1,0:T(8,128)} %cap_in.1), custom_call_target="tpu_custom_call" | custom-call | tf_op jit(solution)/shard_map/pallas_call | solution.py:598
  36.5 0.7 %select_bitcast_fusion = (f32[1,4,64,128]{3,2,1,0:T(8,128)}, f32[1,4,64,128]{3,2,1,0:T(8,128)}) fusion(f32[4,64,128]{2,1,0:T(8,128)S(1)} %get-tuple-element.5, f32[4,64,128]{2,1,0:T(8,128)S(1)} %get-tuple-element.4, pred[]{:T(512)S(6)} %gt.3), kind=kLoop, calls=%fused_computation | loop fusion | flops 65536 | bytes 524289 | tf_op jit(solution)/shard_map/broadcast_in_dim | solution.py:633

commit v11 on v10

--- a/solution.py
+++ b/solution.py
@@ -347,7 +347,12 @@
             (cap.at[pl.ds(start, 2), my_rows], cap.at[pl.ds(start, 2), my_rows], {"tm": span + 1 - 2 * (span % 2)})
             for start in (1, 2 * d + 1)
         ], cap.at[pl.ds(0, 4), pl.ds(0, share)])
-    cap_window = window(cw, cw.at[2], 1, 1), window(cw, cw.at[2], 2, 2)
+    half_block = pl.ds(pl.multiple_of(span % 2 * (share // 2), share // 2), share // 2)
+    half_total = cw.at[pl.ds(0, 2), pl.ds(0, share // 2)]
+    cap_window = window(cw, cw.at[2], 1, 1), batch(
+        [(cw.at[2, half_block], cw.at[2 - k, half_block], beside(k)) for k in (2, -2)], half_total)
+    pass_window = batch(
+        [(cw.at[i, half_block], cw.at[i, half_block], {"tm": span + 1 - 2 * (span % 2)}) for i in (0, 4)], half_total)
     cap2_window = window(kw, kw.at[5], 1, 2), window(kw, kw.at[5], 3, 5)
     gather_r = gather(gr.at[0], gr.at[0, me], range(1, parts)), gather(gr.at[1], r_sent, range(parts), onward)
     c_window = window(vw.at[0], vw.at[0, 3], 1, 3), window(vw.at[1], c_sent, 0, 2, onward)
@@ -375,10 +380,10 @@
     begin(cap2_window[0])
     begin(cap_far)
     begin(far)
+    begin(cap_window[1])
     pl.semaphore_wait(near_sem, 2)
     for k in (2 * NEAR, -2 * NEAR):
         pl.semaphore_signal(far_sem, inc=1, device_id=beside(k), device_id_type=MESH)
-    begin(cap_window[1])
     begin(cap2_window[1])
     cap_sent = dot(pair_rows(cap2), down_cap)
     loads[3].wait()
@@ -489,10 +494,12 @@
     bw[0, 6] = side_by_side(b2)
     pl.semaphore_wait(far_sem, 2)
     begin(gather_r[0])
+    begin(b_window[0])
+    begin(c_window[0])
     arrive(cap_far)
     begin(pass_far)
-    begin(b_window[0])
-    begin(c_window[0])
+    arrive(cap_window[1])
+    begin(pass_window)
     arrive(far)
     arrive(pass_far)
     wide = weights(1, 3 * d - 2)
@@ -508,7 +515,7 @@
     fp_ref[...] = alone
     src1[2:d + 2] = cap[d:2 * d] * alone + src1[2:d + 2]
     begin(known)
-    arrive(cap_window[1])
+    arrive(pass_window)
     a1 = 0.5 * inverse_1(0, 5)[1]
     arrive(cap2_window[1])
     i2 = inverse_2(0, 11)[1]
@@ -622,7 +629,7 @@
             pltpu.VMEM((2, depth, rows, lanes), F32),
             pltpu.SemaphoreType.REGULAR,
             pltpu.SemaphoreType.REGULAR,
-            dma((4,)), dma((18,)), dma((18,)),
+            dma((4,)), dma((19,)), dma((19,)),
         ],
         compiler_params=pltpu.CompilerParams(
             collective_id=0, has_side_effects=True, vmem_limit_bytes=67043328 - 2 * 4 * slab.size

time: 37.3 us -> 37 us (level)
  no operation moved by 1% of the time
where the time goes in v11:
time: 37 us; the launch traced here: 36.9 us
  Pallas kernels  35.6 us (96%)
  other arithmetic  0.72 us (2%)
  between operations  0.64 us (2%)
    pallas_call x1, Pallas kernels, shards(): pl.pallas_call(functools.partial(kernel, parts, spans, steps), out_shape=...  35.6 us

profile of v11, /device:TPU:1, one launch (start us, length us, event | category | flops | bytes accessed | tf_op | source)
XLA Modules:
  0.0 36.9 jit_solution(7660838580768714588)
XLA Ops:
  0.6 35.6 %shard_map.50 = (f32[4,64,128]{2,1,0:T(8,128)S(1)}, f32[4,64,128]{2,1,0:T(8,128)S(1)}) custom-call(f32[4,64,128]{2,1,0:T(8,128)} %bitcast.7, f32[2,4,64,128]{3,2,1,0:T(8,128)} %bitcast.6, f32[4,64,128]{2,1,0:T(8,128)} %cap_in.1), custom_call_target="tpu_custom_call" | custom-call | tf_op jit(solution)/shard_map/pallas_call | solution.py:605
  36.2 0.7 %select_bitcast_fusion = (f32[1,4,64,128]{3,2,1,0:T(8,128)}, f32[1,4,64,128]{3,2,1,0:T(8,128)}) fusion(f32[4,64,128]{2,1,0:T(8,128)S(1)} %get-tuple-element.5, f32[4,64,128]{2,1,0:T(8,128)S(1)} %get-tuple-element.4, pred[]{:T(512)S(6)} %gt.3), kind=kLoop, calls=%fused_computation | loop fusion | flops 65536 | bytes 524289 | tf_op jit(solution)/shard_map/broadcast_in_dim | solution.py:640

commit v12 on v11

--- a/solution.py
+++ b/solution.py
@@ -1,4 +1,5 @@
 import functools
+import math
 
 import jax
 import jax.numpy as jnp
@@ -152,7 +153,7 @@
     parts, spans, steps,
     open_ref, src_ref, cap_in,
     fp_ref, up_ref,
-    u0, src0, src1, cap, c0, c1x, cw, kw, vw, c_sent, bw, b_sent, gr, r_sent, r2s, y3s, own, tmp, fin,
+    u0, src0, src1, cap, c0, c1x, cw, kw, vw, c_sent, bw, b_sent, gr, r_sent, r2s, y3s, own, tmp, fin, spare,
     near_sem, far_sem, in_sem, send_sem, recv_sem,
 ):
     me, span = lax.axis_index("space"), lax.axis_index("tm")
@@ -165,9 +166,9 @@
 
     loads = [
         pltpu.make_async_copy(cap_in, cap.at[pl.ds(depth, depth)], in_sem.at[0]),
-        pltpu.make_async_copy(open_ref, u0, in_sem.at[1]),
-        pltpu.make_async_copy(src_ref.at[0], src0, in_sem.at[2]),
-        pltpu.make_async_copy(src_ref.at[1], src1.at[pl.ds(2, depth)], in_sem.at[3]),
+        pltpu.make_async_copy(open_ref, u0, in_sem.at[0]),
+        pltpu.make_async_copy(src_ref.at[0], src0, in_sem.at[0]),
+        pltpu.make_async_copy(src_ref.at[1], src1.at[pl.ds(2, depth)], in_sem.at[1]),
     ]
     for load in loads:
         load.start()
@@ -285,28 +286,34 @@
         at = start + iota((count, 1, 1), 0)
         return (at >= 0) & (at < of)
 
-    batches = []
-
-    def batch(pieces, total):
-        at = len(batches)
-
-        def copy(source, target, to):
-            return pltpu.make_async_remote_copy(
-                source, target, send_sem.at[at], recv_sem.at[at], device_id=to, device_id_type=MESH)
-
-        made = [copy(*piece) for piece in pieces], copy(total, total, pieces[0][2])
-        batches.append(made)
-        return made
+    own_span, next_span = 0, 1
+    sent_rows, groups_of = [0, 0], {}
+
+    def batch(pieces, total, group=None, side=own_span):
+        at = groups_of.setdefault(group or len(groups_of), len(groups_of))
+        count = total.size // lanes if hasattr(total, "size") else math.prod(total.shape) // lanes
+        sent_rows[side] += count
+        return [
+            pltpu.make_async_remote_copy(
+                source, target, send_sem.at[side], recv_sem.at[at], device_id=to, device_id_type=MESH)
+            for source, target, to in pieces
+        ], count, at, side
+
+    def waiting(count, at, side):
+        rows_of = spare.at[pl.ds(0, count)]
+        return pltpu.make_async_remote_copy(
+            rows_of, rows_of, send_sem.at[side], recv_sem.at[at], device_id=beside(1), device_id_type=MESH)
 
     def begin(made):
         for copy in made[0]:
             copy.start()
 
-    def arrive(made):
-        made[1].wait_recv()
-
-    def sent(made):
-        made[1].wait_send()
+    def arrive(*made):
+        assert len({one[2] for one in made}) == 1
+        waiting(sum(one[1] for one in made), *made[0][2:]).wait_recv()
+
+    def sent(side):
+        waiting(sent_rows[side], 0, side).wait_send()
 
     def beside(k):
         return {"space": lax.rem(me + (k + parts) % parts, parts)}
@@ -321,18 +328,18 @@
         total = buf.at[pl.ds(0, 2 * count)] if rows_at is None else buf.at[pl.ds(0, 2 * count), pl.ds(0, share)]
         return batch([(part(way[0]), part(way[1]), beside(k)) for way, k in ((up, 1), (down, -1))], total)
 
-    def window(buf, source, nearest, reach, to={}):
+    def window(buf, source, nearest, reach, to={}, group=None, side=own_span):
         middle = buf.shape[0] // 2
         offsets = [k for far in range(reach, nearest - 1, -1) for k in ((far, -far) if far else (0,))]
-        return batch([(source, buf.at[middle - k], {**beside(k), **to}) for k in offsets], buf.at[pl.ds(0, len(offsets))])
+        return batch([(source, buf.at[middle - k], {**beside(k), **to}) for k in offsets], buf.at[pl.ds(0, len(offsets))], group, side)
 
     def hops(k):
         z, y = k // 4, k % 4
         return min(z, parts // 4 - z) + min(y, 4 - y)
 
-    def gather(buf, source, offsets, to={}):
+    def gather(buf, source, offsets, to={}, group=None, side=own_span):
         offsets = sorted(offsets, key=lambda k: -hops(k))
-        return batch([(source, buf.at[me], {**beside(k), **to}) for k in offsets], buf.at[pl.ds(0, len(offsets))])
+        return batch([(source, buf.at[me], {**beside(k), **to}) for k in offsets], buf.at[pl.ds(0, len(offsets))], group, side)
 
     d = depth
     onward = {"tm": (span + 1) % spans}
@@ -349,20 +356,20 @@
         ], cap.at[pl.ds(0, 4), pl.ds(0, share)])
     half_block = pl.ds(pl.multiple_of(span % 2 * (share // 2), share // 2), share // 2)
     half_total = cw.at[pl.ds(0, 2), pl.ds(0, share // 2)]
-    cap_window = window(cw, cw.at[2], 1, 1), batch(
+    cap_window = window(cw, cw.at[2], 1, 1, group="first"), batch(
         [(cw.at[2, half_block], cw.at[2 - k, half_block], beside(k)) for k in (2, -2)], half_total)
     pass_window = batch(
         [(cw.at[i, half_block], cw.at[i, half_block], {"tm": span + 1 - 2 * (span % 2)}) for i in (0, 4)], half_total)
-    cap2_window = window(kw, kw.at[5], 1, 2), window(kw, kw.at[5], 3, 5)
-    gather_r = gather(gr.at[0], gr.at[0, me], range(1, parts)), gather(gr.at[1], r_sent, range(parts), onward)
-    c_window = window(vw.at[0], vw.at[0, 3], 1, 3), window(vw.at[1], c_sent, 0, 2, onward)
-    b_window = window(bw.at[0], bw.at[0, 6], 1, 6), window(bw.at[1], b_sent, 0, 6, onward)
-    fin_onward = batch([(fin.at[0], fin.at[1], onward)], fin.at[0])
-
-    loads[0].wait()
+    cap2_window = window(kw, kw.at[5], 1, 2, group="first"), window(kw, kw.at[5], 3, 5)
+    to_next = {"to": onward, "group": "next", "side": next_span}
+    gather_r = gather(gr.at[0], gr.at[0, me], range(1, parts), group="own"), gather(gr.at[1], r_sent, range(parts), **to_next)
+    c_window = window(vw.at[0], vw.at[0, 3], 1, 3, group="own"), window(vw.at[1], c_sent, 0, 2, **to_next)
+    b_window = window(bw.at[0], bw.at[0, 6], 1, 6, group="own"), window(bw.at[1], b_sent, 0, 6, **to_next)
+    fin_onward = batch([(fin.at[0], fin.at[1], onward)], fin.at[0], "next", next_span)
+
+    loaded = spare.at[pl.ds(0, 3 * depth * rows)]
+    pltpu.make_async_copy(loaded, loaded, in_sem.at[0]).wait()
     mine = cap[d:2 * d]
-    loads[1].wait()
-    loads[2].wait()
     b = mine * u0[...] + src0[...]
     own[...] = b
     c0[d + 1:2 * d + 1] = b * (W / (mine + 6.0))
@@ -409,6 +416,8 @@
 
     arrive(cap_near)
     a = weights(d - 1, d + 2)
+
+    assert len(groups_of) == 13 and max(sent_rows) <= spare.shape[0]
 
     def first_sweeps(b, c, a):
         x = 1.2 * c[1:-1] + a * sum_inner(c, lanes)
@@ -482,8 +491,7 @@
 
     arrive(near)
     x, b1 = first_sweeps(own[...], planes_of(c0, d + 1, d - 1, d + 4), a)
-    arrive(cap_window[0])
-    arrive(cap2_window[0])
+    arrive(cap_window[0], cap2_window[0])
     d1, i1 = inverse_1(1, 4)
     d2, i2 = inverse_2(3, 8)
     near_1 = i1, d1, 0.5 * i1, i2, d2, 0.25 * i2
@@ -520,9 +528,7 @@
     arrive(cap2_window[1])
     i2 = inverse_2(0, 11)[1]
     a2 = 0.25 * i2[1:-1]
-    arrive(gather_r[0])
-    arrive(b_window[0])
-    arrive(c_window[0])
+    arrive(gather_r[0], b_window[0], c_window[0])
 
     got = gr[0]
     cap3 = capacity_3(got)
@@ -565,10 +571,7 @@
     def _():
         begin(fin_onward)
 
-    handed = gather_r[1], b_window[1], c_window[1], fin_onward
-    for made in batches:
-        if not any(made is other for other in handed):
-            sent(made)
+    sent(own_span)
 
     @pl.when(span == 0)
     def _():
@@ -576,10 +579,7 @@
 
     @pl.when(span > 0)
     def _():
-        arrive(handed[0])
-        arrive(handed[1])
-        arrive(handed[2])
-        arrive(handed[3])
+        arrive(gather_r[1], b_window[1], c_window[1], fin_onward)
         c1 = jnp.where(valid(me - 2, 5, parts), vw[1, 1:6], 0.0)
         y1 = 1.2 * c1 + a1 * sum_packed(c1, half)
         y1 = (0.2 * y1 + c1) + a1 * sum_packed(y1, half)
@@ -590,8 +590,7 @@
 
     @pl.when(span < spans - 1)
     def _():
-        for made in handed:
-            sent(made)
+        sent(next_span)
 
 
 def shards(span_opening, source_power, warmth_retention):
@@ -627,9 +626,10 @@
             pltpu.VMEM((depth, rows, lanes), F32),
             pltpu.VMEM((12 * rows, lanes), F32),
             pltpu.VMEM((2, depth, rows, lanes), F32),
+            pltpu.VMEM((2048, lanes), F32),
             pltpu.SemaphoreType.REGULAR,
             pltpu.SemaphoreType.REGULAR,
-            dma((4,)), dma((19,)), dma((19,)),
+            dma((2,)), dma((2,)), dma((13,)),
         ],
         compiler_params=pltpu.CompilerParams(
             collective_id=0, has_side_effects=True, vmem_limit_bytes=67043328 - 2 * 4 * slab.size

time: 37 us -> 36.8 us (level)
  no operation moved by 1% of the time
where the time goes in v12:
time: 36.8 us; the launch traced here: 36.7 us
  Pallas kernels  35.3 us (96%)
  other arithmetic  0.72 us (2%)
  between operations  0.64 us (2%)
    pallas_call x1, Pallas kernels, shards(): pl.pallas_call(functools.partial(kernel, parts, spans, steps), out_shape=...  35.3 us

profile of v12, /device:TPU:1, one launch (start us, length us, event | category | flops | bytes accessed | tf_op | source)
XLA Modules:
  0.0 36.7 jit_solution(2802167961409677352)
XLA Ops:
  0.6 35.3 %shard_map.50 = (f32[4,64,128]{2,1,0:T(8,128)S(1)}, f32[4,64,128]{2,1,0:T(8,128)S(1)}) custom-call(f32[4,64,128]{2,1,0:T(8,128)} %bitcast.7, f32[2,4,64,128]{3,2,1,0:T(8,128)} %bitcast.6, f32[4,64,128]{2,1,0:T(8,128)} %cap_in.1), custom_call_target="tpu_custom_call" | custom-call | tf_op jit(solution)/shard_map/pallas_call | solution.py:604
  36.0 0.7 %select_bitcast_fusion = (f32[1,4,64,128]{3,2,1,0:T(8,128)}, f32[1,4,64,128]{3,2,1,0:T(8,128)}) fusion(f32[4,64,128]{2,1,0:T(8,128)S(1)} %get-tuple-element.5, f32[4,64,128]{2,1,0:T(8,128)S(1)} %get-tuple-element.4, pred[]{:T(512)S(6)} %gt.3), kind=kLoop, calls=%fused_computation | loop fusion | flops 65536 | bytes 524289 | tf_op jit(solution)/shard_map/broadcast_in_dim | solution.py:640

commit v13 on v12

--- a/solution.py
+++ b/solution.py
@@ -321,12 +321,12 @@
     share = rows // 2
     my_rows = pl.ds(pl.multiple_of(span % 2 * share, share), share)
 
-    def halo(buf, count, up, down, rows_at=None):
+    def halo(buf, count, up, down, rows_at=None, group=None):
         def part(start):
             return buf.at[pl.ds(start, count)] if rows_at is None else buf.at[pl.ds(start, count), rows_at]
 
         total = buf.at[pl.ds(0, 2 * count)] if rows_at is None else buf.at[pl.ds(0, 2 * count), pl.ds(0, share)]
-        return batch([(part(way[0]), part(way[1]), beside(k)) for way, k in ((up, 1), (down, -1))], total)
+        return batch([(part(way[0]), part(way[1]), beside(k)) for way, k in ((up, 1), (down, -1))], total, group)
 
     def window(buf, source, nearest, reach, to={}, group=None, side=own_span):
         middle = buf.shape[0] // 2
@@ -343,11 +343,11 @@
 
     d = depth
     onward = {"tm": (span + 1) % spans}
-    near = halo(c0, 2, (2 * d - 1, d - 1), (d + 1, 2 * d + 1))
+    near = halo(c0, 2, (2 * d - 1, d - 1), (d + 1, 2 * d + 1), group="near")
     far = halo(c0, 1, (2 * d - 2, d - 2), (d + 3, 2 * d + 3))
     known = halo(src1, 2, (d, 0), (2, d + 2))
     third = halo(c1x, 1, (d, 0), (5, d + 5))
-    cap_near = halo(cap, 1, (2 * d - 1, d - 1), (d, 2 * d))
+    cap_near = halo(cap, 1, (2 * d - 1, d - 1), (d, 2 * d), group="near")
     cap_far = halo(cap, 2, (d + 1, 1), (d + 1, 2 * d + 1), my_rows)
     pass_far = batch(
         [
@@ -386,8 +386,8 @@
     kw[5] = cap2[0, :rows // 8] + pltpu.roll(cap2[0, rows // 8:], GROUP, 1)
     begin(cap2_window[0])
     begin(cap_far)
+    begin(cap_window[1])
     begin(far)
-    begin(cap_window[1])
     pl.semaphore_wait(near_sem, 2)
     for k in (2 * NEAR, -2 * NEAR):
         pl.semaphore_signal(far_sem, inc=1, device_id=beside(k), device_id_type=MESH)
@@ -414,10 +414,10 @@
         diagonal = jnp.concatenate([packed, pltpu.roll(packed, lanes - GROUP, 2)], 1) + 1.5
         return diagonal, jnp.where(iota(diagonal.shape, 2) < GROUP, inverse(diagonal, start, 5), 0.0)
 
-    arrive(cap_near)
+    arrive(cap_near, near)
     a = weights(d - 1, d + 2)
 
-    assert len(groups_of) == 13 and max(sent_rows) <= spare.shape[0]
+    assert len(groups_of) == 12 and max(sent_rows) <= spare.shape[0]
 
     def first_sweeps(b, c, a):
         x = 1.2 * c[1:-1] + a * sum_inner(c, lanes)
@@ -489,7 +489,6 @@
         total = (sides + up_down(lift))[1:-1] + (lift[:-2] + lift[2:])
         return 0.2 * lift[1:-1] + a * total
 
-    arrive(near)
     x, b1 = first_sweeps(own[...], planes_of(c0, d + 1, d - 1, d + 4), a)
     arrive(cap_window[0], cap2_window[0])
     d1, i1 = inverse_1(1, 4)
@@ -629,7 +628,7 @@
             pltpu.VMEM((2048, lanes), F32),
             pltpu.SemaphoreType.REGULAR,
             pltpu.SemaphoreType.REGULAR,
-            dma((2,)), dma((2,)), dma((13,)),
+            dma((2,)), dma((2,)), dma((12,)),
         ],
         compiler_params=pltpu.CompilerParams(
             collective_id=0, has_side_effects=True, vmem_limit_bytes=67043328 - 2 * 4 * slab.size

time: 36.8 us -> 36.7 us (level)
  no operation moved by 1% of the time
where the time goes in v13:
time: 36.7 us; the launch traced here: 36.6 us
  Pallas kernels  35.3 us (96%)
  other arithmetic  0.72 us (2%)
  between operations  0.64 us (2%)
    pallas_call x1, Pallas kernels, shards(): pl.pallas_call(functools.partial(kernel, parts, spans, steps), out_shape=...  35.3 us

profile of v13, /device:TPU:1, one launch (start us, length us, event | category | flops | bytes accessed | tf_op | source)
XLA Modules:
  0.0 36.6 jit_solution(12125507534731937742)
XLA Ops:
  0.6 35.3 %shard_map.50 = (f32[4,64,128]{2,1,0:T(8,128)S(1)}, f32[4,64,128]{2,1,0:T(8,128)S(1)}) custom-call(f32[4,64,128]{2,1,0:T(8,128)} %bitcast.7, f32[2,4,64,128]{3,2,1,0:T(8,128)} %bitcast.6, f32[4,64,128]{2,1,0:T(8,128)} %cap_in.1), custom_call_target="tpu_custom_call" | custom-call | tf_op jit(solution)/shard_map/pallas_call | solution.py:603
  35.9 0.7 %select_bitcast_fusion = (f32[1,4,64,128]{3,2,1,0:T(8,128)}, f32[1,4,64,128]{3,2,1,0:T(8,128)}) fusion(f32[4,64,128]{2,1,0:T(8,128)S(1)} %get-tuple-element.5, f32[4,64,128]{2,1,0:T(8,128)S(1)} %get-tuple-element.4, pred[]{:T(512)S(6)} %gt.3), kind=kLoop, calls=%fused_computation | loop fusion | flops 65536 | bytes 524289 | tf_op jit(solution)/shard_map/broadcast_in_dim | solution.py:639

commit v14 on v13

--- a/solution.py
+++ b/solution.py
@@ -344,7 +344,7 @@
     d = depth
     onward = {"tm": (span + 1) % spans}
     near = halo(c0, 2, (2 * d - 1, d - 1), (d + 1, 2 * d + 1), group="near")
-    far = halo(c0, 1, (2 * d - 2, d - 2), (d + 3, 2 * d + 3))
+    far = halo(c0, 1, (2 * d - 2, d - 2), (d + 3, 2 * d + 3), group="far")
     known = halo(src1, 2, (d, 0), (2, d + 2))
     third = halo(c1x, 1, (d, 0), (5, d + 5))
     cap_near = halo(cap, 1, (2 * d - 1, d - 1), (d, 2 * d), group="near")
@@ -353,7 +353,7 @@
         [
             (cap.at[pl.ds(start, 2), my_rows], cap.at[pl.ds(start, 2), my_rows], {"tm": span + 1 - 2 * (span % 2)})
             for start in (1, 2 * d + 1)
-        ], cap.at[pl.ds(0, 4), pl.ds(0, share)])
+        ], cap.at[pl.ds(0, 4), pl.ds(0, share)], "far")
     half_block = pl.ds(pl.multiple_of(span % 2 * (share // 2), share // 2), share // 2)
     half_total = cw.at[pl.ds(0, 2), pl.ds(0, share // 2)]
     cap_window = window(cw, cw.at[2], 1, 1, group="first"), batch(
@@ -417,7 +417,7 @@
     arrive(cap_near, near)
     a = weights(d - 1, d + 2)
 
-    assert len(groups_of) == 12 and max(sent_rows) <= spare.shape[0]
+    assert len(groups_of) == 11 and max(sent_rows) <= spare.shape[0]
 
     def first_sweeps(b, c, a):
         x = 1.2 * c[1:-1] + a * sum_inner(c, lanes)
@@ -507,8 +507,7 @@
     begin(pass_far)
     arrive(cap_window[1])
     begin(pass_window)
-    arrive(far)
-    arrive(pass_far)
+    arrive(far, pass_far)
     wide = weights(1, 3 * d - 2)
     c = planes_of(c0, d + 1, d - 2, d + 6)
     first = 1.2 * c[1:2] + wide[1:2] * sum_inner(c[0:3], lanes)
@@ -628,7 +627,7 @@
             pltpu.VMEM((2048, lanes), F32),
             pltpu.SemaphoreType.REGULAR,
             pltpu.SemaphoreType.REGULAR,
-            dma((2,)), dma((2,)), dma((12,)),
+            dma((2,)), dma((2,)), dma((11,)),
         ],
         compiler_params=pltpu.CompilerParams(
             collective_id=0, has_side_effects=True, vmem_limit_bytes=67043328 - 2 * 4 * slab.size

time: 36.7 us -> 36.7 us (level)
  no operation moved by 1% of the time
where the time goes in v14:
time: 36.7 us; the launch traced here: 36.6 us
  Pallas kernels  35.2 us (96%)
  other arithmetic  0.72 us (2%)
  between operations  0.64 us (2%)
    pallas_call x1, Pallas kernels, shards(): pl.pallas_call(functools.partial(kernel, parts, spans, steps), out_shape=...  35.2 us

profile of v14, /device:TPU:1, one launch (start us, length us, event | category | flops | bytes accessed | tf_op | source)
XLA Modules:
  0.0 36.6 jit_solution(15317675099732086977)
XLA Ops:
  0.6 35.2 %shard_map.50 = (f32[4,64,128]{2,1,0:T(8,128)S(1)}, f32[4,64,128]{2,1,0:T(8,128)S(1)}) custom-call(f32[4,64,128]{2,1,0:T(8,128)} %bitcast.7, f32[2,4,64,128]{3,2,1,0:T(8,128)} %bitcast.6, f32[4,64,128]{2,1,0:T(8,128)} %cap_in.1), custom_call_target="tpu_custom_call" | custom-call | tf_op jit(solution)/shard_map/pallas_call | solution.py:602
  35.9 0.7 %select_bitcast_fusion = (f32[1,4,64,128]{3,2,1,0:T(8,128)}, f32[1,4,64,128]{3,2,1,0:T(8,128)}) fusion(f32[4,64,128]{2,1,0:T(8,128)S(1)} %get-tuple-element.5, f32[4,64,128]{2,1,0:T(8,128)S(1)} %get-tuple-element.4, pred[]{:T(512)S(6)} %gt.3), kind=kLoop, calls=%fused_computation | loop fusion | flops 65536 | bytes 524289 | tf_op jit(solution)/shard_map/broadcast_in_dim | solution.py:638
